TPU v7x, 32 devices: a 4x4x1 block of a 4x4x8 slice. The times are simulated.
32 devices in a mesh: rep: 1 (over z), model: 32 (over y, x, core).
Axes of the slice: x: 4, y: 4, z: 1, core: 2. Of those that a mesh axis runs over, the one named last changes fastest.
The devices are a block of a 4x4x8 slice.
Arguments:
- acts_in: bfloat16 [8192, 512], P('rep')
- w_first: bfloat16 [1024, 512], P(('rep', 'model'))
- w_middle: bfloat16 [1024, 1024], P(('rep', 'model'))
- w_last: bfloat16 [1024, 1024], P(('rep', 'model'))
- u_first: float32 [1024], P(('rep', 'model'))
- u_middle: float32 [1024], P(('rep', 'model'))
- u_last: float32 [1024], P(('rep', 'model'))
- target: bfloat16 [8192, 1024], P('rep', 'model')
Outputs:
- output 1: float32 [1], P('rep')
- output 2: bfloat16 [8192, 512], P('rep')
- output 3: float32 [1024, 512], P(('rep', 'model'))
- output 4: float32 [1024, 1024], P(('rep', 'model'))
- output 5: float32 [1024, 1024], P(('rep', 'model'))
- output 6: float32 [1024], P(('rep', 'model'))
- output 7: float32 [1024], P(('rep', 'model'))
- output 8: float32 [1024], P(('rep', 'model'))
- output 9: bfloat16 [512], P('rep')
- output 10: bfloat16 [1024], P('rep')
- output 11: bfloat16 [1024], P('rep')
- output 12: float32 [3], P('rep')
All inputs are finite; a program needn't handle non-finite values.
Results may differ from a plain program's by a relative error of at most 0.02.
Values are sent between devices in bfloat16 or wider.
A program may use at most 768 MiB of HBM per device.

v0:
```python
import jax
import jax.numpy as jnp
from jax import lax
from jax.sharding import PartitionSpec as P

LEAK = 0.2
NORM_FLOOR = 1e-12
POWER_STEPS = 2
ROW_DIMS = (((1,), (1,)), ((), ()))
BATCH_DIMS = (((0,), (0,)), ((), ()))


def power_steps(w_local, u_local):
    u_vec = u_local
    for step_index in range(POWER_STEPS):
        p_vec = lax.psum(jnp.dot(u_vec.astype(jnp.bfloat16), w_local, preferred_element_type=jnp.float32), "model")
        v_vec = (p_vec / jnp.maximum(jnp.sqrt(jnp.sum(p_vec * p_vec)), NORM_FLOOR)).astype(jnp.bfloat16)
        s_local = jnp.dot(w_local, v_vec, preferred_element_type=jnp.float32)
        sigma_val = jnp.sqrt(lax.psum(jnp.sum(s_local * s_local), "model"))
        u_vec = s_local / sigma_val
    return u_vec, v_vec, sigma_val


def device_program(acts_in, w_first, w_middle, w_last, u_first, u_middle, u_last, target):
    weights = (w_first, w_middle, w_last)
    u_starts = (u_first, u_middle, u_last)
    row_count = acts_in.shape[0]
    powered = []
    layer_in = [acts_in]
    layer_out = []
    for layer in range(3):
        u_new, v_vec, sigma_val = power_steps(weights[layer], u_starts[layer])
        powered.append((u_new, v_vec, sigma_val))
        y_local = lax.dot_general(layer_in[layer], weights[layer], ROW_DIMS, preferred_element_type=jnp.float32) / sigma_val
        layer_out.append(y_local)
        if layer < 2:
            act_local = jax.nn.leaky_relu(y_local, LEAK).astype(jnp.bfloat16)
            layer_in.append(lax.all_gather(act_local, "model", axis=1, tiled=True))
    residual = layer_out[2] - target.astype(jnp.float32)
    loss_value = lax.psum(jnp.sum(residual * residual), "model") * (0.5 / row_count)
    grad_y = residual / row_count
    weight_grads = [None, None, None]
    grad_in = None
    for layer in (2, 1, 0):
        u_new, v_vec, sigma_val = powered[layer]
        grad_low = grad_y.astype(jnp.bfloat16)
        grad_mat = lax.dot_general(grad_low, layer_in[layer], BATCH_DIMS, preferred_element_type=jnp.float32)
        corr_sum = lax.psum(jnp.sum(grad_y * layer_out[layer]), "model")
        weight_grads[layer] = (grad_mat - corr_sum * jnp.outer(u_new, v_vec.astype(jnp.float32))) / sigma_val
        share_in = (jnp.dot(grad_low, weights[layer], preferred_element_type=jnp.float32) / sigma_val).astype(jnp.bfloat16)
        if layer > 0:
            grad_act = lax.psum_scatter(share_in, "model", scatter_dimension=1, tiled=True)
            grad_y = grad_act.astype(jnp.float32) * jnp.where(layer_out[layer - 1] >= 0, 1.0, LEAK)
        else:
            grad_in = lax.psum(share_in, "model")
    sigmas = jnp.stack([powered[0][2], powered[1][2], powered[2][2]])
    return (loss_value.reshape(1), grad_in, weight_grads[0], weight_grads[1], weight_grads[2], powered[0][0], powered[1][0], powered[2][0], powered[0][1], powered[1][1], powered[2][1], sigmas)


def solution(mesh):
    row_spec = P("rep", None)
    weight_spec = P(("rep", "model"), None)
    vector_spec = P(("rep", "model"))
    group_spec = P("rep")
    in_specs = (row_spec, weight_spec, weight_spec, weight_spec, vector_spec, vector_spec, vector_spec, P("rep", "model"))
    out_specs = (group_spec, row_spec, weight_spec, weight_spec, weight_spec, vector_spec, vector_spec, vector_spec, group_spec, group_spec, group_spec, group_spec)
    return jax.shard_map(device_program, mesh=mesh, in_specs=in_specs, out_specs=out_specs, check_vma=False)
```

profile of v0, /device:TPU:97, one launch (start us, length us, event | category | flops | bytes accessed | tf_op | source)
XLA Modules:
  0.0 733.4 jit_solution(8734965251061145980)
XLA Ops:
  7.2 0.1 all-gather.3.cloned.1.call-start
  7.3 1.0 fusion.11
  8.3 0.8 fusion.15
  9.0 0.9 fusion.19
  9.9 49.9 %all-reduce.4 = (f32[512]{0:T(512)S(1)}, f32[1024]{0:T(1024)S(1)}, f32[1024]{0:T(1024)S(1)}) all-reduce(f32[512]{0:T(512)S(1)} %bitcast.75, f32[1024]{0:T(1024)S(1)} %bitcast.73, f32[1024]{0:T(1024)S(1)} %bitcast.72), channel_id=1, replica_groups=mesh['rep'=1,'model'=32] {'model'}, use_global_device_ids=true, to_apply=%region_0.0 | all-reduce | flops 2560 | bytes 20480 | tf_op jit(solution)/shard_map/psum | solution.py:16
  59.8 0.6 multiply_reduce_fusion.7
  61.1 0.6 multiply_reduce_fusion.5
  62.4 0.7 multiply_reduce_fusion.13
  63.2 1.6 multiply_reduce_fusion.11
  64.7 0.6 multiply_reduce_fusion.9
  66.1 1.5 multiply_reduce_fusion.15
  67.5 43.6 %all-reduce.3 = (f32[]{:T(128)}, f32[]{:T(128)}, f32[]{:T(128)}) all-reduce(f32[]{:T(128)} %get-tuple-element.36, f32[]{:T(128)} %get-tuple-element.38, f32[]{:T(128)} %get-tuple-element.40), channel_id=1, replica_groups=mesh['rep'=1,'model'=32] {'model'}, use_global_device_ids=true, to_apply=%region_3.0 | all-reduce | flops 3 | bytes 24 | tf_op jit(solution)/shard_map/psum | solution.py:19
  113.2 1.0 fusion.9
  114.2 0.1 fusion.13
  114.3 0.9 fusion.17
  115.2 43.9 %all-reduce.2 = (f32[512]{0:T(512)S(1)}, f32[1024]{0:T(1024)S(1)}, f32[1024]{0:T(1024)S(1)}) all-reduce(f32[512]{0:T(512)S(1)} %bitcast.74, f32[1024]{0:T(1024)S(1)} %bitcast.71, f32[1024]{0:T(1024)S(1)} %bitcast.70), channel_id=1, replica_groups=mesh['rep'=1,'model'=32] {'model'}, use_global_device_ids=true, to_apply=%region_4.0 | all-reduce | flops 2560 | bytes 20480 | tf_op jit(solution)/shard_map/psum | solution.py:16
  159.1 0.6 multiply_reduce_fusion.4
  160.4 1.6 multiply_reduce_fusion.10
  162.0 0.6 multiply_reduce_fusion.6
  163.3 0.7 multiply_reduce_fusion.12
  164.1 0.6 multiply_reduce_fusion.8
  165.4 1.5 multiply_reduce_fusion.14
  166.9 44.7 %all-reduce.1 = (f32[]{:T(128)}, f32[]{:T(128)}, f32[]{:T(128)}) all-reduce(f32[]{:T(128)} %get-tuple-element.42, f32[]{:T(128)} %get-tuple-element.44, f32[]{:T(128)} %get-tuple-element.46), channel_id=1, replica_groups=mesh['rep'=1,'model'=32] {'model'}, use_global_device_ids=true, to_apply=%region_7.0 | all-reduce | flops 3 | bytes 24 | tf_op jit(solution)/shard_map/psum | solution.py:19
  212.3 6.8 fusion.5
  219.2 0.1 all-gather.5.cloned.1.call-start
  219.9 65.3 %all-gather.3.cloned.1.call-done = bf16[8192,1024]{0,1:T(8,128)(2,1)} async-done(((bf16[8192,32]{0,1:T(8,128)(2,1)}), bf16[8192,1024]{0,1:T(8,128)(2,1)}) %all-gather.3.cloned.1.call-update) | async-done | bytes 16777232 | tf_op jit(solution)/shard_map/all_gather | solution.py:38
  285.2 9.6 %fusion.6 = (bf16[8192,32]{0,1:T(8,128)(2,1)}, f32[8192,32]{0,1:T(8,128)S(1)}) fusion(f32[]{:T(128)} %sqrt.43, bf16[32,1024]{1,0:T(8,128)(2,1)S(1)} %copy-done, bf16[8192,1024]{0,1:T(8,128)(2,1)} %all-gather.3.cloned.1.call-done), kind=kOutput, calls=%fused_computation.25 | convolution fusion | flops 538181632 | bytes 18415620 | tf_op jit(solution)/shard_map/dot_general | solution.py:34
  294.9 0.1 all-gather.5.cloned.1.call-update
  294.9 0.2 reduce-scatter.3.cloned.1.call-start
  295.9 65.9 %all-gather.5.cloned.1.call-done = bf16[8192,1024]{0,1:T(8,128)(2,1)} async-done(((bf16[8192,32]{0,1:T(8,128)(2,1)}), bf16[8192,1024]{0,1:T(8,128)(2,1)}) %all-gather.5.cloned.1.call-update) | async-done | bytes 16777232 | tf_op jit(solution)/shard_map/all_gather | solution.py:38
  361.8 9.4 %multiply_reduce_fusion = (f32[]{:T(128)}, f32[]{:T(128)}, f32[8192,32]{0,1:T(8,128)S(1)}) fusion(bf16[8192,32]{0,1:T(8,128)(2,1)S(1)} %copy-done.5, f32[]{:T(128)} %sqrt.47, bf16[32,1024]{1,0:T(8,128)(2,1)S(1)} %copy-done.6, bf16[8192,1024]{0,1:T(8,128)(2,1)} %all-gather.5.cloned.1.call-done), kind=kOutput, calls=%fused_computation.26 | convolution fusion | flops 538968064 | bytes 18415628 | tf_op jit(solution)/shard_map/dot_general | solution.py:34
  371.1 1.0 copy-done.3
  372.1 8.2 %divide_convert_fusion.1 = bf16[8192,1024]{0,1:T(8,128)(2,1)} fusion(f32[]{:T(128)} %sqrt.47, bf16[32,1024]{1,0:T(8,128)(2,1)S(1)} %copy-done.6, f32[8192,32]{0,1:T(8,128)S(1)} %get-tuple-element.52, bf16[8192,32]{0,1:T(8,128)(2,1)S(1)} %copy-done.5), kind=kOutput, calls=%fused_computation.1 | convolution fusion | flops 554696704 | bytes 18415620 | tf_op jit(solution)/shard_map/dot_general | solution.py:50
  380.3 0.1 reduce-scatter.5.cloned.1.call-start
  380.4 105.0 %reduce-scatter.3.cloned.1.call-done = bf16[8192,32]{0,1:T(8,128)(2,1)} async-done(((bf16[8192,1024]{0,1:T(8,128)(2,1)}), bf16[8192,32]{0,1:T(8,128)(2,1)}) %reduce-scatter.3.cloned.1.call-update) | async-done | bytes 524304 | tf_op jit(solution)/shard_map/reduce_scatter | solution.py:52
  485.4 9.1 %divide_convert_fusion = bf16[8192,1024]{0,1:T(8,128)(2,1)} fusion(f32[]{:T(128)} %sqrt.43, bf16[32,1024]{1,0:T(8,128)(2,1)S(1)} %copy-done, f32[8192,32]{0,1:T(8,128)S(1)} %get-tuple-element.51, bf16[8192,32]{0,1:T(8,128)(2,1)} %reduce-scatter.3.cloned.1.call-done), kind=kOutput, calls=%fused_computation | convolution fusion | flops 554958848 | bytes 18415620 | tf_op jit(solution)/shard_map/dot_general | solution.py:50
  494.6 0.1 all-reduce.7.cloned.1.call-start
  494.6 107.0 %reduce-scatter.5.cloned.1.call-done = bf16[8192,32]{0,1:T(8,128)(2,1)} async-done(((bf16[8192,1024]{0,1:T(8,128)(2,1)}), bf16[8192,32]{0,1:T(8,128)(2,1)}) %reduce-scatter.5.cloned.1.call-update) | async-done | bytes 524304 | tf_op jit(solution)/shard_map/reduce_scatter | solution.py:52
  601.7 5.8 divide_convert_fusion.2
  607.5 0.6 pad_maximum_fusion
  608.2 1.9 multiply_reduce_fusion.1
  610.1 0.9 multiply_reduce_fusion.2
  611.0 47.0 %all-reduce = (f32[]{:T(128)}, f32[]{:T(128)}, f32[]{:T(128)}, f32[]{:T(128)}) all-reduce(f32[]{:T(128)} %get-tuple-element.13, f32[]{:T(128)} %multiply_reduce_fusion.2, f32[]{:T(128)} %multiply_reduce_fusion.1, f32[]{:T(128)} %get-tuple-element.12), channel_id=1, replica_groups=mesh['rep'=1,'model'=32] {'model'}, use_global_device_ids=true, to_apply=%region_25.26 | all-reduce | flops 4 | bytes 32 | tf_op jit(solution)/shard_map/psum | solution.py:40
  658.6 6.0 fusion.2
  664.7 12.3 %fusion.1 = f32[32,1024]{1,0:T(8,128)} fusion(bf16[8192,1024]{0,1:T(8,128)(2,1)} %all-gather.3.cloned.1.call-done, f32[]{:T(128)} %sqrt.43, f32[1024]{0:T(1024)S(1)} %get-tuple-element.32, f32[32]{0:T(128)S(1)} %broadcast_divide_fusion.1, f32[]{:T(128)} %get-tuple-element.16, f32[8192,32]{0,1:T(8,128)S(1)} %get-tuple-element.51, ...), kind=kOutput, calls=%fused_computation.13 | convolution fusion | flops 538312704 | bytes 18485384 | tf_op jit(solution)/shard_map/dot_general | solution.py:47
  677.0 12.1 %fusion = f32[32,1024]{1,0:T(8,128)} fusion(bf16[8192,1024]{0,1:T(8,128)(2,1)} %all-gather.5.cloned.1.call-done, f32[]{:T(128)} %sqrt.47, f32[1024]{0:T(1024)S(1)} %get-tuple-element.30, f32[32]{0:T(128)S(1)} %broadcast_divide_fusion, f32[]{:T(128)} %get-tuple-element.17, f32[8192,32]{0,1:T(8,128)S(1)} %copy-done.4, bf16[8192,32]{0,1:T(8,128)(2,1)S(1)} %copy-done.5), kind=kOutput, calls=%fused_computation.11 | convolution fusion | flops 538050560 | bytes 18485384 | tf_op jit(solution)/shard_map/dot_general | solution.py:47
  689.1 29.3 %all-reduce.7.cloned.1.call-done = bf16[8192,512]{1,0:T(8,128)(2,1)} async-done(((bf16[8192,512]{1,0:T(8,128)(2,1)}), bf16[8192,512]{1,0:T(8,128)(2,1)}) %all-reduce.7.cloned.1.call-update) | async-done | bytes 8388624 | tf_op jit(solution)/shard_map/psum | solution.py:55
  718.4 7.3 copy.21
  (45 shorter events, 0.4 us)
Async XLA Ops:
  7.2 1.1 copy-start
  7.2 278.0 %all-gather.3.cloned.1.call-start = ((), (), s32[]{:S(2)}) async-start(), calls=%async_computation.2 | async-start | bytes 17301504 | tf_op jit(solution)/shard_map/all_gather | solution.py:38
  160.4 134.4 %copy-start.8 = (bf16[1024]{0:T(1024)(128)(2,1)}, bf16[1024]{0:T(1024)(128)(2,1)S(1)}, u32[]{:S(2)}) copy-start(bf16[1024]{0:T(1024)(128)(2,1)S(1)} %get-tuple-element.65) | copy-start | bytes 6148
  163.3 131.5 %copy-start.9 = (bf16[1024]{0:T(1024)(128)(2,1)}, bf16[1024]{0:T(1024)(128)(2,1)S(1)}, u32[]{:S(2)}) copy-start(bf16[1024]{0:T(1024)(128)(2,1)S(1)} %get-tuple-element.64) | copy-start | bytes 6148
  165.4 129.5 %copy-start.10 = (bf16[512]{0:T(512)(128)(2,1)}, bf16[512]{0:T(512)(128)(2,1)S(1)}, u32[]{:S(2)}) copy-start(bf16[512]{0:T(512)(128)(2,1)S(1)} %get-tuple-element.63) | copy-start | bytes 3076
  212.3 149.4 %copy-start.5 = (bf16[8192,32]{0,1:T(8,128)(2,1)S(1)}, bf16[8192,32]{0,1:T(8,128)(2,1)}, u32[]{:S(2)}) copy-start(bf16[8192,32]{0,1:T(8,128)(2,1)} %param.15) | copy-start | bytes 1572868
  212.3 149.4 %copy-start.6 = (bf16[32,1024]{1,0:T(8,128)(2,1)S(1)}, bf16[32,1024]{1,0:T(8,128)(2,1)}, u32[]{:S(2)}) copy-start(bf16[32,1024]{1,0:T(8,128)(2,1)} %param.11) | copy-start | bytes 196612
  219.2 142.6 %all-gather.5.cloned.1.call-start = ((), (), s32[]{:S(2)}) async-start(), calls=%async_computation.3 | async-start | bytes 17301504 | tf_op jit(solution)/shard_map/all_gather | solution.py:38
  294.9 190.5 %reduce-scatter.3.cloned.1.call-start = ((), (), s32[]{:S(2)}) async-start(), calls=%async_computation.4 | async-start | bytes 17301504 | tf_op jit(solution)/shard_map/reduce_scatter | solution.py:52
  371.1 1.0 copy-start.3
  380.3 221.3 %reduce-scatter.5.cloned.1.call-start = ((), (), s32[]{:S(2)}) async-start(), calls=%async_computation.5 | async-start | bytes 17301504 | tf_op jit(solution)/shard_map/reduce_scatter | solution.py:52
  494.5 107.1 %copy-start.7 = (bf16[32,512]{1,0:T(8,128)(2,1)S(1)}, bf16[32,512]{1,0:T(8,128)(2,1)}, u32[]{:S(2)}) copy-start(bf16[32,512]{1,0:T(8,128)(2,1)} %param.9) | copy-start | bytes 98308
  494.6 223.8 %all-reduce.7.cloned.1.call-start = ((), (), s32[]{:S(2)}) async-start(), calls=%async_computation.6 | async-start | bytes 16777216 | tf_op jit(solution)/shard_map/psum | solution.py:55
  601.7 8.4 %copy-start.2 = (bf16[8192,32]{0,1:T(8,128)(2,1)S(1)}, bf16[8192,32]{0,1:T(8,128)(2,1)}, u32[]{:S(2)}) copy-start(bf16[8192,32]{0,1:T(8,128)(2,1)} %reduce-scatter.5.cloned.1.call-done) | copy-start | bytes 1572868
  608.1 68.9 %copy-start.11 = (f32[32]{0:T(128)}, f32[32]{0:T(128)S(1)}, u32[]{:S(2)}) copy-start(f32[32]{0:T(128)S(1)} %broadcast_divide_fusion.1) | copy-start | bytes 388
  608.1 68.8 %copy-start.13 = (f32[32]{0:T(128)}, f32[32]{0:T(128)S(1)}, u32[]{:S(2)}) copy-start(f32[32]{0:T(128)S(1)} %broadcast_divide_fusion.2) | copy-start | bytes 388
  608.1 68.8 %copy-start.12 = (f32[32]{0:T(128)}, f32[32]{0:T(128)S(1)}, u32[]{:S(2)}) copy-start(f32[32]{0:T(128)S(1)} %broadcast_divide_fusion) | copy-start | bytes 388
  664.7 12.3 %copy-start.4 = (f32[8192,32]{0,1:T(8,128)S(1)}, f32[8192,32]{0,1:T(8,128)}, u32[]{:S(2)}) copy-start(f32[8192,32]{0,1:T(8,128)} %copy-done.3) | copy-start | bytes 3145732
  677.0 48.8 %copy-start.1 = (bf16[32,1024]{1,0:T(8,128)(2,1)S(1)}, bf16[32,1024]{1,0:T(8,128)(2,1)}, u32[]{:S(2)}) copy-start(bf16[32,1024]{1,0:T(8,128)(2,1)} %param.10) | copy-start | bytes 196612
Sparse Core Ops, SparseCore 0:
  219.3 65.9 all-gather.2
  295.0 66.6 all-gather.4
  380.4 104.8 reduce-scatter.2
  494.7 106.9 reduce-scatter.4
  607.6 110.7 all-reduce.6
where the time goes:
time: 735 us; the launch traced here: 733 us
  waiting for transfers between devices  373 us (51%)
  blocking collectives  229 us (31%)
  matrix products  91.5 us (12%)
  between operations  24.1 us (3%)
  local copies, waits for them, and re-layouts  8.41 us (1%)
    reduce_scatter x2, waiting for transfers between devices, device_program(): lax.psum_scatter(share_in, 'model', scatter_dimension=1, tiled=True)  212 us
    all_gather x2, waiting for transfers between devices, device_program(): layer_in.append(lax.all_gather(act_local, 'model', axis=1, tiled=True))  131 us
    psum x2, blocking collectives, power_steps(): lax.psum(jnp.dot(u_vec.astype(jnp.bfloat16), w_local, preferred_element_t...  93.8 us
    psum x2, blocking collectives, power_steps(): sigma_val = jnp.sqrt(lax.psum(jnp.sum(s_local * s_local), 'model'))  88.3 us
    psum x1, blocking collectives, device_program(): lax.psum(jnp.sum(residual * residual), 'model') * (0.5 / row_count)  47 us
    dot_general x3, matrix products, device_program(): lax.dot_general(grad_low, layer_in[layer], BATCH_DIMS, preferred_element_...  30.5 us
    psum x1, waiting for transfers between devices, device_program(): grad_in = lax.psum(share_in, 'model')  29.3 us
    dot_general x3, matrix products, device_program(): lax.dot_general(layer_in[layer], weights[layer], ROW_DIMS, preferred_elem...  25.7 us
  transfers between devices with their start and end apart: 5, of which 5 were waited for; matrix products, arithmetic and copies ran while one was open for 5% of the time, Pallas kernels for 0%

commit v1 on v0

v1 whole, which is shorter than its diff:
```python
import jax
import jax.numpy as jnp
from jax import lax
from jax.sharding import PartitionSpec as P

LEAK = 0.2
NORM_FLOOR = 1e-12
POWER_STEPS = 2
ROW_DIMS = (((1,), (1,)), ((), ()))
BATCH_DIMS = (((0,), (0,)), ((), ()))


def power_steps(weight, u_vec):
    for step_index in range(POWER_STEPS):
        p_vec = jnp.dot(u_vec.astype(jnp.bfloat16), weight, preferred_element_type=jnp.float32)
        v_vec = (p_vec / jnp.maximum(jnp.sqrt(jnp.sum(p_vec * p_vec)), NORM_FLOOR)).astype(jnp.bfloat16)
        s_vec = jnp.dot(weight, v_vec, preferred_element_type=jnp.float32)
        sigma_val = jnp.sqrt(jnp.sum(s_vec * s_vec))
        u_vec = s_vec / sigma_val
    return u_vec, v_vec, sigma_val


def device_program(acts_in, w_first, w_middle, w_last, u_first, u_middle, u_last, target):
    n = lax.axis_size("model")
    me = lax.axis_index("model")
    row_count = acts_in.shape[0]
    rows = row_count // n
    weights = [lax.all_gather(w, "model", axis=0, tiled=True) for w in (w_first, w_middle, w_last)]
    u_rows = u_first.shape[0]
    u_all = lax.all_gather(jnp.stack([u_first, u_middle, u_last]), "model", axis=1, tiled=True)
    target_rows = lax.all_to_all(target, "model", split_axis=0, concat_axis=1, tiled=True)
    layer_in = [lax.dynamic_slice_in_dim(acts_in, me * rows, rows, 0)]
    layer_out = []
    powered = []
    for layer in range(3):
        powered.append(power_steps(weights[layer], u_all[layer]))
        y_local = lax.dot_general(layer_in[layer], weights[layer], ROW_DIMS, preferred_element_type=jnp.float32) / powered[layer][2]
        layer_out.append(y_local)
        if layer < 2:
            layer_in.append(jax.nn.leaky_relu(y_local, LEAK).astype(jnp.bfloat16))
    residual = layer_out[2] - target_rows.astype(jnp.float32)
    loss_value = lax.psum(jnp.sum(residual * residual), "model") * (0.5 / row_count)
    grad_y = residual / row_count
    weight_grads = [None, None, None]
    grad_in = None
    for layer in (2, 1, 0):
        u_new, v_vec, sigma_val = powered[layer]
        grad_low = grad_y.astype(jnp.bfloat16)
        grad_mat = lax.dot_general(grad_low, layer_in[layer], BATCH_DIMS, preferred_element_type=jnp.float32)
        corr_sum = jnp.sum(grad_y * layer_out[layer])
        share = (grad_mat - corr_sum * jnp.outer(u_new, v_vec.astype(jnp.float32))) / sigma_val
        weight_grads[layer] = lax.psum_scatter(share, "model", scatter_dimension=0, tiled=True)
        grad_act = (jnp.dot(grad_low, weights[layer], preferred_element_type=jnp.float32) / sigma_val).astype(jnp.bfloat16)
        if layer > 0:
            grad_y = grad_act.astype(jnp.float32) * jnp.where(layer_out[layer - 1] >= 0, 1.0, LEAK)
        else:
            grad_in = lax.all_gather(grad_act, "model", axis=0, tiled=True)
    sigmas = jnp.stack([powered[0][2], powered[1][2], powered[2][2]])
    u_next = [lax.dynamic_slice_in_dim(entry[0], me * u_rows, u_rows, 0) for entry in powered]
    return (loss_value.reshape(1), grad_in, weight_grads[0], weight_grads[1], weight_grads[2], u_next[0], u_next[1], u_next[2], powered[0][1], powered[1][1], powered[2][1], sigmas)


def solution(mesh):
    row_spec = P("rep", None)
    weight_spec = P(("rep", "model"), None)
    vector_spec = P(("rep", "model"))
    group_spec = P("rep")
    in_specs = (row_spec, weight_spec, weight_spec, weight_spec, vector_spec, vector_spec, vector_spec, P("rep", "model"))
    out_specs = (group_spec, row_spec, weight_spec, weight_spec, weight_spec, vector_spec, vector_spec, vector_spec, group_spec, group_spec, group_spec, group_spec)
    return jax.shard_map(device_program, mesh=mesh, in_specs=in_specs, out_specs=out_specs, check_vma=False)
```

time: 735 us -> 446 us (0.61)
  blocking collectives: 229 us -> 74.1 us
  waiting for transfers between devices: 373 us -> 276 us
  matrix products: 91.5 us -> 36.9 us
  starting transfers between devices: 0.5 us -> 9.76 us
    psum x4 -> x0, blocking collectives: 182 us -> none  [the longest x2 93.8 us: power_steps(): lax.psum(jnp.dot(u_vec.astype(jnp.bfloat16), w_local, preferred_element_t...]
    all_gather x2 -> x4, waiting for transfers between devices: 131 us -> 60 us  [the longest x3 60 us: device_program(): lax.all_gather(w, 'model', axis=0, tiled=True)]
    psum x1 -> x0, waiting for transfers between devices: 29.3 us -> none  [device_program(): grad_in = lax.psum(share_in, 'model')]
    all_gather x0 -> x1, blocking collectives: none -> 28.9 us  [device_program(): lax.all_gather(jnp.stack([u_first, u_middle, u_last]), 'model', axis=1, t...]
    dot_general x3, matrix products: 30.5 us -> 10.8 us  [device_program(): lax.dot_general(grad_low, layer_in[layer], BATCH_DIMS, preferred_element_...]
    dot_general x3, matrix products: 25.7 us -> 6.12 us  [device_program(): lax.dot_general(layer_in[layer], weights[layer], ROW_DIMS, preferred_elem...]
    dot_general x3, matrix products: 23.1 us -> 4.02 us  [device_program(): jnp.dot(grad_low, weights[layer], preferred_element_type=jnp.float32)]
    all_to_all x0 -> x1, starting transfers between devices: none -> 9.14 us  [device_program(): lax.all_to_all(target, 'model', split_axis=0, concat_axis=1, tiled=True)]
  transfers between devices with their start and end apart: 5 -> 8, of which waited for: 5 -> 6; matrix products, arithmetic and copies ran while one was open for 5% -> 7% of each run, Pallas kernels for 0% -> 0%
where the time goes in v1:
time: 446 us; the launch traced here: 445 us
  waiting for transfers between devices  276 us (62%)
  blocking collectives  74.1 us (17%)
  matrix products  36.9 us (8%)
  between operations  24.6 us (6%)
  local copies, waits for them, and re-layouts  15.6 us (3%)
  starting transfers between devices  9.76 us (2%)
  other arithmetic  8.16 us (2%)
    reduce_scatter x3, waiting for transfers between devices, device_program(): lax.psum_scatter(share, 'model', scatter_dimension=0, tiled=True)  213 us
    all_gather x3, waiting for transfers between devices, device_program(): lax.all_gather(w, 'model', axis=0, tiled=True)  60 us
    psum x1, blocking collectives, device_program(): lax.psum(jnp.sum(residual * residual), 'model') * (0.5 / row_count)  45.2 us
    all_gather x1, blocking collectives, device_program(): lax.all_gather(jnp.stack([u_first, u_middle, u_last]), 'model', axis=1, t...  28.9 us
    dot_general x3, matrix products, device_program(): lax.dot_general(grad_low, layer_in[layer], BATCH_DIMS, preferred_element_...  10.8 us
    unnamed x39, local copies, waits for them, and re-layouts  10.5 us
    all_to_all x1, starting transfers between devices, device_program(): lax.all_to_all(target, 'model', split_axis=0, concat_axis=1, tiled=True)  9.14 us
  transfers between devices with their start and end apart: 8, of which 6 were waited for; matrix products, arithmetic and copies ran while one was open for 7% of the time, Pallas kernels for 0%

profile of v1, /device:TPU:97, one launch (start us, length us, event | category | flops | bytes accessed | tf_op | source)
XLA Modules:
  0.0 444.9 jit_solution(5820673581270485997)
XLA Ops:
  7.3 0.7 all-gather.6.cloned.1.call-update
  8.1 0.7 all-gather.8.cloned.1.call-update
  8.8 1.9 copy.36
  10.7 9.1 %all-to-all-start = ((bf16[32,256,32]{1,2,0:T(8,128)(2,1)}), bf16[32,256,32]{1,2,0:T(8,128)(2,1)S(1)}, u32[]{:S(2)}, u32[]{:S(2)}) async-start(bf16[32,256,32]{1,2,0:T(8,128)(2,1)} %bitcast.74), calls=%async_computation | async-start | bytes 1048576 | tf_op jit(solution)/shard_map/all_to_all | solution.py:31
  19.9 0.7 all-gather.10.cloned.1.call-update
  20.8 28.9 %all-gather = bf16[32,32,3]{1,2,0:T(4,128)(2,1)S(1)} all-gather(bf16[1,32,3]{1,2,0:T(4,128)(2,1)S(1)} %maximum_bitcast_fusion), channel_id=1, replica_groups=mesh['rep'=1,'model'=32] {'model'}, dimensions={0}, use_global_device_ids=true | all-gather | bytes 6336 | tf_op jit(solution)/shard_map/all_gather | solution.py:30
  49.9 1.3 copy.31
  51.2 1.1 all-gather.6.cloned.1.call-done
  52.4 1.5 fusion.21
  53.9 0.6 multiply_reduce_fusion.15
  55.2 1.6 fusion.35
  56.8 0.6 multiply_reduce_fusion.13
  58.4 0.6 multiply_reduce_fusion.14
  60.1 0.6 multiply_reduce_fusion.12
  61.4 2.4 convolution_divide_fusion
  63.9 28.3 %all-gather.8.cloned.1.call-done = bf16[1024,1024]{1,0:T(8,128)(2,1)} async-done(((bf16[32,1024]{1,0:T(8,128)(2,1)}), bf16[1024,1024]{1,0:T(8,128)(2,1)}) %all-gather.8.cloned.1.call-update) | async-done | bytes 2097168 | tf_op jit(solution)/shard_map/all_gather | solution.py:28
  92.2 2.1 fusion.20
  94.3 0.6 multiply_reduce_fusion.11
  95.6 0.6 fusion.38
  96.3 0.6 multiply_reduce_fusion.10
  98.0 0.6 multiply_reduce_fusion.9
  99.3 0.6 fusion.40
  100.0 0.6 multiply_reduce_fusion.8
  101.3 30.5 %all-gather.10.cloned.1.call-done = bf16[1024,1024]{1,0:T(8,128)(2,1)} async-done(((bf16[32,1024]{1,0:T(8,128)(2,1)}), bf16[1024,1024]{1,0:T(8,128)(2,1)}) %all-gather.10.cloned.1.call-update) | async-done | bytes 2097168 | tf_op jit(solution)/shard_map/all_gather | solution.py:28
  131.8 2.0 fusion.19
  133.8 0.6 multiply_reduce_fusion.7
  135.1 2.2 fusion.41
  137.3 0.6 multiply_reduce_fusion.6
  138.7 2.0 fusion.42
  140.7 0.6 multiply_reduce_fusion.5
  142.0 2.2 fusion.43
  144.2 0.6 multiply_reduce_fusion.4
  145.6 2.2 convolution_divide_fusion.4
  147.8 1.6 multiply_reduce_fusion
  149.3 1.4 multiply_reduce_fusion.1
  150.8 1.4 multiply_reduce_fusion.2
  152.2 0.9 copy-done.10
  153.1 1.1 fusion.6
  154.4 3.7 subtract_divide_fusion.2
  158.2 1.1 copy-done.14
  159.4 3.5 subtract_divide_fusion
  163.3 0.9 copy-done.12
  164.3 3.6 subtract_divide_fusion.1
  168.6 45.2 %psum.7 = f32[]{:T(128)} all-reduce(f32[]{:T(128)} %get-tuple-element.13), channel_id=1, replica_groups=mesh['rep'=1,'model'=32] {'model'}, use_global_device_ids=true, to_apply=%region_13.14 | all-reduce | flops 1 | bytes 8 | tf_op jit(solution)/shard_map/psum | solution.py:42
  216.2 57.6 %reduce-scatter.4.cloned.1.call-done = f32[32,512]{1,0:T(8,128)} async-done(((f32[1024,512]{1,0:T(8,128)}), f32[32,512]{1,0:T(8,128)}) %reduce-scatter.4.cloned.1.call-update) | async-done | bytes 65552 | tf_op jit(solution)/shard_map/reduce_scatter | solution.py:52
  273.8 77.9 %reduce-scatter.8.cloned.1.call-done = f32[32,1024]{1,0:T(8,128)} async-done(((f32[1024,1024]{1,0:T(8,128)}), f32[32,1024]{1,0:T(8,128)}) %reduce-scatter.8.cloned.1.call-update) | async-done | bytes 131088 | tf_op jit(solution)/shard_map/reduce_scatter | solution.py:52
  351.6 78.0 %reduce-scatter.6.cloned.1.call-done = f32[32,1024]{1,0:T(8,128)} async-done(((f32[1024,1024]{1,0:T(8,128)}), f32[32,1024]{1,0:T(8,128)}) %reduce-scatter.6.cloned.1.call-update) | async-done | bytes 131088 | tf_op jit(solution)/shard_map/reduce_scatter | solution.py:52
  429.6 7.3 %copy.38 = bf16[8192,512]{1,0:T(8,128)(2,1)} copy(bf16[8192,512]{1,0:T(8,128)(2,1)} %all-gather.12.cloned.1.call-done) | data formatting | bytes 16777216
  (80 shorter events, 4.8 us)
Async XLA Ops:
  7.2 13.6 %copy-start.9 = (f32[32]{0:T(128)S(1)}, f32[32]{0:T(128)}, u32[]{:S(2)}) copy-start(f32[32]{0:T(128)} %param.12) | copy-start | bytes 388
  7.2 13.6 %copy-start.8 = (f32[32]{0:T(128)S(1)}, f32[32]{0:T(128)}, u32[]{:S(2)}) copy-start(f32[32]{0:T(128)} %param.13) | copy-start | bytes 388
  7.2 13.6 %copy-start.7 = (f32[32]{0:T(128)S(1)}, f32[32]{0:T(128)}, u32[]{:S(2)}) copy-start(f32[32]{0:T(128)} %param.14) | copy-start | bytes 388
  7.2 45.1 %all-gather.6.cloned.1.call-start = ((), (), s32[]{:S(2)}) async-start(), calls=%async_computation.4 | async-start | bytes 1081344 | tf_op jit(solution)/shard_map/all_gather | solution.py:28
  8.0 84.1 %all-gather.8.cloned.1.call-start = ((), (), s32[]{:S(2)}) async-start(), calls=%async_computation.5 | async-start | bytes 2162688 | tf_op jit(solution)/shard_map/all_gather | solution.py:28
  10.7 39.1 %all-to-all-start = ((bf16[32,256,32]{1,2,0:T(8,128)(2,1)}), bf16[32,256,32]{1,2,0:T(8,128)(2,1)S(1)}, u32[]{:S(2)}, u32[]{:S(2)}) async-start(bf16[32,256,32]{1,2,0:T(8,128)(2,1)} %bitcast.74), calls=%async_computation | async-start | bytes 1048576 | tf_op jit(solution)/shard_map/all_to_all | solution.py:31
  19.9 112.0 %all-gather.10.cloned.1.call-start = ((), (), s32[]{:S(2)}) async-start(), calls=%async_computation.6 | async-start | bytes 2162688 | tf_op jit(solution)/shard_map/all_gather | solution.py:28
  20.7 195.5 %all-gather.12.cloned.1.call-start = ((), (), s32[]{:S(2)}) async-start(), calls=%async_computation.7 | async-start | bytes 8650752 | tf_op jit(solution)/shard_map/all_gather | solution.py:57
  52.4 5.8 %copy-start.2 = (bf16[1024,512]{1,0:T(8,128)(2,1)S(1)}, bf16[1024,512]{1,0:T(8,128)(2,1)}, u32[]{:S(2)}) copy-start(bf16[1024,512]{1,0:T(8,128)(2,1)} %all-gather.6.cloned.1.call-done) | copy-start | bytes 3145732
  59.7 4.1 copy-start.6
  92.2 3.5 copy-start
  99.3 34.5 %copy-start.4 = (bf16[1024]{0:T(1024)(128)(2,1)}, bf16[1024]{0:T(1024)(128)(2,1)S(1)}, u32[]{:S(2)}) copy-start(bf16[1024]{0:T(1024)(128)(2,1)S(1)} %get-tuple-element.50) | copy-start | bytes 6148
  142.0 5.8 %copy-start.5 = (bf16[1024]{0:T(1024)(128)(2,1)}, bf16[1024]{0:T(1024)(128)(2,1)S(1)}, u32[]{:S(2)}) copy-start(bf16[1024]{0:T(1024)(128)(2,1)S(1)} %get-tuple-element.51) | copy-start | bytes 6148
  145.5 2.2 copy-start.1
  145.6 2.2 copy-start.3
  147.8 1.6 copy-start.13
  149.3 1.5 copy-start.17
  149.3 1.5 copy-start.11
  150.8 1.4 copy-start.15
  152.2 0.9 copy-start.10
  154.3 119.5 %reduce-scatter.4.cloned.1.call-start = ((), (), s32[]{:S(2)}) async-start(), calls=%async_computation.8 | async-start | bytes 2162688 | tf_op jit(solution)/shard_map/reduce_scatter | solution.py:52
  158.1 1.2 copy-start.14
  158.1 1.4 copy-start.18
  158.1 193.5 %reduce-scatter.8.cloned.1.call-start = ((), (), s32[]{:S(2)}) async-start(), calls=%async_computation.10 | async-start | bytes 4325376 | tf_op jit(solution)/shard_map/reduce_scatter | solution.py:52
  163.0 1.2 copy-start.12
  163.0 1.4 copy-start.16
  163.0 266.6 %reduce-scatter.6.cloned.1.call-start = ((), (), s32[]{:S(2)}) async-start(), calls=%async_computation.9 | async-start | bytes 4325376 | tf_op jit(solution)/shard_map/reduce_scatter | solution.py:52
Sparse Core Ops, SparseCore 0:
  10.1 42.1 all-gather.5
  54.4 37.6 all-gather.7
  94.3 37.5 all-gather.9
  154.4 47.0 all-gather.11
  205.3 68.4 reduce-scatter.3
  277.7 73.9 reduce-scatter.7
  355.7 73.8 reduce-scatter.5

commit v2 on v0

v2 whole, which is shorter than its diff:
```python
import math

import jax
import jax.numpy as jnp
from jax import lax
from jax.experimental import pallas as pl
from jax.experimental.pallas import tpu as pltpu
from jax.sharding import PartitionSpec as P

LEAK = 0.2
NORM_FLOOR = 1e-12
POWER_STEPS = 2
MESH = pl.DeviceIdType.MESH
F32 = jnp.float32
BF16 = jnp.bfloat16
NN = (((1,), (0,)), ((), ()))
NT = (((1,), (1,)), ((), ()))
TN = (((0,), (0,)), ((), ()))
CORES = 2
LANES = 128
SUB = 16
TILE = 256
AG_SEMS = 72
RS_SEMS = 20
TG_SEMS = 28
DX_PARTS = 2
XP, XM, YP, YM = (1, 0), (-1, 0), (0, 1), (0, -1)


def dot(lhs, rhs, dims):
    return lax.dot_general(lhs, rhs, dims, preferred_element_type=F32)


class Place:
    def __init__(self, n):
        self.side = math.isqrt(n // CORES)
        me = lax.axis_index("model")
        self.me = me
        self.core = lax.rem(me, CORES)
        self.x = lax.rem(me // CORES, self.side)
        self.y = me // (CORES * self.side)

    def col(self, dx):
        return lax.rem(self.x + (dx + self.side), self.side)

    def row(self, dy):
        return lax.rem(self.y + (dy + self.side), self.side)

    def dev(self, rel, other=False):
        core = 1 - self.core if other else self.core
        return (self.row(rel[1]) * self.side + self.col(rel[0])) * CORES + core

    def norm(self, rel):
        s = self.side
        half = s // 2
        return tuple((r + half - 1) % s - (half - 1) for r in rel)


class Chan:
    def __init__(self, place, send_sems, recv_sems):
        self.place, self.send_sems, self.recv_sems = place, send_sems, recv_sems
        self.index, self.sent = {}, []

    def copy(self, key, src, dst, target):
        i = self.index.setdefault(key, len(self.index))
        return pltpu.make_async_remote_copy(
            src_ref=src, dst_ref=dst, send_sem=self.send_sems.at[i], recv_sem=self.recv_sems.at[i],
            device_id={"model": target}, device_id_type=MESH)

    def start(self, key, src, dst, target):
        desc = self.copy(key, src, dst, target)
        desc.start()
        self.sent.append(desc)

    def wait(self, key, dst):
        self.copy(key, dst, dst, self.place.dev((0, 0), True)).wait_recv()

    def drain(self):
        for desc in self.sent:
            desc.wait_send()
        self.sent = []


class Gather:
    def __init__(self, chan, ref_at, cuts, pair=True):
        self.chan, self.ref_at, self.pair = chan, ref_at, pair
        self.place = chan.place
        a, b, c, d, e = cuts
        keep = lambda *spans: [s for s in spans if s[1] > s[0]]
        self.full, self.mid, self.outer = keep((a, e)), keep((b, d)), keep((a, b), (d, e))
        self.half = {"x": keep((a, c)), "y": keep((c, e))}
        self.fwd = {"x": keep((b, c)), "y": keep((c, d))}
        self.bwd = {"x": keep((a, b)), "y": keep((d, e))}

    def start(self, rel, spans, way):
        rel = self.place.norm(rel)
        for s in spans:
            ref = self.ref_at(self.place.dev(rel), s)
            self.chan.start((rel, s, way), ref, ref, self.place.dev(way))

    def wait(self, rel, spans, way):
        rel = self.place.norm(rel)
        src = self.place.norm((rel[0] + way[0], rel[1] + way[1]))
        src = self.place.norm((rel[0] + way[0], rel[1] + way[1]))
        for s in spans:
            self.chan.wait((src, s, way), self.ref_at(self.place.dev(rel), s))

    def mate(self, *rels):
        if self.pair:
            for rel in rels:
                ref = self.ref_at(self.place.dev(rel), self.full[0])
                self.chan.start((rel, "mate"), ref, ref, self.place.dev((0, 0), True))

    def both(self, rel, spans, axis):
        for way in ((XP, XM) if axis == "x" else (YP, YM)):
            self.start(rel, spans, way)

    def step0(self):
        for way in (XP, XM, YP, YM):
            self.start((0, 0), self.full, way)
        self.mate((0, 0))

    def step1(self):
        for way in (XP, YP, XM, YM):
            rel = (-way[0], -way[1])
            self.wait(rel, self.full, way)
            self.start(rel, self.mid if way in (XP, YP) else self.outer, way)
            if way[0]:
                self.both(rel, self.half["x"], "y")
            else:
                self.both(rel, self.half["y"], "x")
            self.mate(rel)

    def hop(self, rel, axis):
        first = "x" if axis == "y" else "y"
        off = rel[1] if axis == "y" else rel[0]
        way = {("y", -1): YP, ("y", 1): YM, ("x", -1): XP, ("x", 1): XM}[(axis, off)]
        self.wait(rel, self.half[first], way)
        self.start(rel, (self.fwd if off < 0 else self.bwd)[first], way)

    def end(self, rel, axis):
        first = "x" if axis == "y" else "y"
        self.wait(rel, self.fwd[first], YP if axis == "y" else XP)
        self.wait(rel, self.bwd[first], YM if axis == "y" else XM)

    def step2(self):
        for d in (-1, 1):
            for e in (-1, 1):
                self.hop((d, e), "y")
                self.hop((e, d), "x")
        self.mate((-1, -1), (-1, 1), (1, -1), (1, 1))
        self.wait((2, 0), self.mid, XP)
        self.wait((2, 0), self.outer, XM)
        self.both((2, 0), self.half["x"], "y")
        self.wait((0, 2), self.mid, YP)
        self.wait((0, 2), self.outer, YM)
        self.both((0, 2), self.half["y"], "x")
        self.mate((2, 0), (0, 2))

    def step3(self):
        for d in (-1, 1):
            self.hop((2, d), "y")
            self.hop((d, 2), "x")
        for d in (-1, 1):
            self.end((d, 2), "y")
            self.end((2, d), "x")
        self.mate((-1, 2), (1, 2), (2, -1), (2, 1))

    def step4(self):
        self.end((2, 2), "y")
        self.end((2, 2), "x")
        self.mate((2, 2))

    def finish(self):
        if self.pair:
            r = range(-1, self.place.side - 1)
            for rel in [(dx, dy) for dx in r for dy in r]:
                self.chan.wait((rel, "mate"), self.ref_at(self.place.dev(rel, True), self.full[0]))


class Reduce:
    def __init__(self, chan, blocks, mate, relay, main, relay2, main2, acc, width):
        self.chan, self.place = chan, chan.place
        self.blocks, self.mate = blocks, mate
        self.relay, self.main, self.relay2, self.main2, self.acc = relay, main, relay2, main2, acc
        q = width // 4
        self.q = q
        self.cols = {"x": ((q, 2 * q), (0, q), (0, 2 * q)), "y": ((2 * q, 3 * q), (3 * q, 4 * q), (2 * q, 4 * q))}

    def at(self, axis, pos, span):
        cols = pl.ds(span[0], span[1] - span[0])
        if axis == "x":
            return self.blocks.at[:, pos, self.place.core, :, cols]
        return self.blocks.at[pos, :, self.place.core, :, cols]

    def one(self, dx, dy, span):
        return self.blocks.at[self.place.row(dy), self.place.col(dx), self.place.core, :, pl.ds(span[0], span[1] - span[0])]

    def pair_send(self):
        p = self.place
        self.chan.start("pair", self.blocks.at[:, :, 1 - p.core], self.mate, p.dev((0, 0), True))

    def pair_add(self):
        p = self.place
        self.chan.wait("pair", self.mate)
        for k in range(p.side):
            mine = self.blocks.at[k, :, p.core]
            mine[...] = (mine[...].astype(F32) + self.mate[k].astype(F32)).astype(BF16)

    def pos(self, axis, d):
        return self.place.col(d) if axis == "x" else self.place.row(d)

    def ways(self, axis):
        return (XP, XM) if axis == "x" else (YP, YM)

    def far_send(self):
        for h, axis in enumerate(("x", "y")):
            for s, way in enumerate(self.ways(axis)):
                self.chan.start(("far", h, s), self.at(axis, self.pos(axis, 2), self.cols[axis][s]),
                                self.relay.at[h, s], self.place.dev(way))

    def far_add(self):
        for h, axis in enumerate(("x", "y")):
            for s, way in enumerate(self.ways(axis)):
                self.chan.wait(("far", h, s), self.relay.at[h, s])
                step = 1 if s == 0 else -1
                ref = self.at(axis, self.pos(axis, step), self.cols[axis][s])
                ref[...] = (ref[...].astype(F32) + self.relay[h, s].astype(F32)).astype(BF16)
                self.chan.start(("near", h, s), self.at(axis, self.pos(axis, step), self.cols[axis][2]),
                                self.main.at[h, s], self.place.dev(way))

    def near_add(self):
        p = self.place
        for h, (axis, cross) in enumerate((("x", "y"), ("y", "x"))):
            for s in range(2):
                self.chan.wait(("near", h, s), self.main.at[h, s])
            own = self.pos(cross, 0)
            span = self.cols[axis][2]
            self.acc[h] = (self.one(0, 0, span)[...].astype(F32) + self.main[h, 0, own].astype(F32)
                           + self.main[h, 1, own].astype(F32))
            ref = self.at(axis, self.pos(axis, 0), span)
            ref[...] = (ref[...].astype(F32) + self.main[h, 0].astype(F32) + self.main[h, 1].astype(F32)).astype(BF16)
            for s, way in enumerate(self.ways(cross)):
                d = (0, 2) if cross == "y" else (2, 0)
                self.chan.start(("far2", h, s), self.one(d[0], d[1], self.cols[axis][s]),
                                self.relay2.at[h, s], p.dev(way))

    def far2_add(self):
        p = self.place
        for h, (axis, cross) in enumerate((("x", "y"), ("y", "x"))):
            for s, way in enumerate(self.ways(cross)):
                self.chan.wait(("far2", h, s), self.relay2.at[h, s])
                ref = self.one(way[0], way[1], self.cols[axis][s])
                ref[...] = (ref[...].astype(F32) + self.relay2[h, s].astype(F32)).astype(BF16)
                self.chan.start(("near2", h, s), self.one(way[0], way[1], self.cols[axis][2]),
                                self.main2.at[h, s], p.dev(way))

    def finish(self, out_ref, inv):
        for h in range(2):
            for s in range(2):
                self.chan.wait(("near2", h, s), self.main2.at[h, s])
            out_ref[:, pl.ds(2 * self.q * h, 2 * self.q)] = (
                self.acc[h] + self.main2[h, 0].astype(F32) + self.main2[h, 1].astype(F32)) * inv


class Spread:
    def __init__(self, chan, mine, stage, relay, mid, final):
        self.chan, self.place = chan, chan.place
        self.mine, self.stage, self.relay, self.mid, self.final = mine, stage, relay, mid, final

    def pair_send(self):
        p = self.place
        self.chan.start("pair", self.mine.at[1 - p.core], self.stage.at[p.core], p.dev((0, 0), True))

    def pair_take(self):
        p = self.place
        self.stage[p.core] = self.mine[p.core]
        self.chan.wait("pair", self.stage.at[1 - p.core])

    def src(self, h, pos, lo, hi):
        rest = pl.ds(lo, hi - lo)
        return self.stage.at[h, rest, pos] if h == 0 else self.stage.at[h, pos, rest]

    def first_send(self):
        p = self.place
        s2 = p.side // 2
        for h in range(2):
            here = p.x if h == 0 else p.y
            ways = (XP, XM) if h == 0 else (YP, YM)
            pos = p.col if h == 0 else p.row
            for s, way in enumerate(ways):
                self.chan.start(("far", h, s), self.src(h, pos(2), s * s2, s * s2 + s2), self.relay.at[h, s], p.dev(way))
            for s, way in enumerate(ways):
                d = 1 if s == 0 else -1
                self.chan.start(("near", h, s), self.src(h, pos(d), 0, p.side), self.mid.at[h, here], p.dev(way))
            self.mid[h, here] = self.src(h, here, 0, p.side)[...]

    def first_relay(self):
        p = self.place
        s2 = p.side // 2
        for h in range(2):
            ways = (XP, XM) if h == 0 else (YP, YM)
            pos = p.col if h == 0 else p.row
            for s, way in enumerate(ways):
                self.chan.wait(("far", h, s), self.relay.at[h, s])
                self.chan.start(("on", h, s), self.relay.at[h, s],
                                self.mid.at[h, pos(-1 if s == 0 else 1), pl.ds(s * s2, s2)], p.dev(way))

    def second_send(self):
        p = self.place
        s2 = p.side // 2
        for h in range(2):
            pos = p.col if h == 0 else p.row
            for s in range(2):
                self.chan.wait(("near", h, s), self.mid.at[h, pos(-1 if s == 0 else 1)])
                self.chan.wait(("on", h, s), self.mid.at[h, pos(2), pl.ds(s * s2, s2)])
            cross = p.row if h == 0 else p.col
            ways = (YP, YM) if h == 0 else (XP, XM)
            for s, way in enumerate(ways):
                self.chan.start(("far2", h, s), self.mid.at[h, pl.ds(s * s2, s2), cross(2)],
                                self.relay.at[2 + h, s], p.dev(way))
            for s, way in enumerate(ways):
                self.chan.start(("near2", h, s), self.mid.at[h, :, cross(1 if s == 0 else -1)],
                                self.dst(h, cross(0), 0, p.side), p.dev(way))
            self.dst(h, cross(0), 0, p.side)[...] = self.mid[h, :, cross(0)]

    def dst(self, h, pos, lo, hi):
        rest = pl.ds(lo, hi - lo)
        return self.final.at[pos, rest, h] if h == 0 else self.final.at[rest, pos, h]

    def second_relay(self):
        p = self.place
        s2 = p.side // 2
        for h in range(2):
            cross = p.row if h == 0 else p.col
            ways = (YP, YM) if h == 0 else (XP, XM)
            for s, way in enumerate(ways):
                self.chan.wait(("far2", h, s), self.relay.at[2 + h, s])
                self.chan.start(("on2", h, s), self.relay.at[2 + h, s],
                                self.dst(h, cross(-1 if s == 0 else 1), s * s2, s * s2 + s2), p.dev(way))

    def finish(self):
        p = self.place
        s2 = p.side // 2
        for h in range(2):
            cross = p.row if h == 0 else p.col
            for s in range(2):
                self.chan.wait(("near2", h, s), self.dst(h, cross(-1 if s == 0 else 1), 0, p.side))
                self.chan.wait(("on2", h, s), self.dst(h, cross(2), s * s2, s * s2 + s2))


def row_of(value, rows):
    return jnp.broadcast_to(value, (rows, value.shape[1]))


def split3(value):
    hi = value.astype(BF16)
    rest = value - hi.astype(F32)
    mid = rest.astype(BF16)
    lo = (rest - mid.astype(F32)).astype(BF16)
    return hi, mid, lo


def kernel(n, acts_hbm, w0_hbm, w1_hbm, w2_hbm, u0_ref, u1_ref, u2_ref, target_hbm,
           loss_ref, dx_ref, g0_ref, g1_ref, g2_ref, un0_ref, un1_ref, un2_ref, v0_ref, v1_ref, v2_ref, sig_ref,
           w0, w1, w2, x0, x1, x2, y0, y1, y2, grad, low, sq,
           tbuf, tmine, tstage, trelay, tmid, tfinal, lossbuf, losspair,
           d0, d1, d2, m0, m1, m2,
           ra0, rb0, rc0, re0, rf0, ra1, rb1, rc1, re1, rf1, ra2, rb2, rc2, re2, rf2,
           local_sems, w_send, w_recv, dx_send, dx_recv, rs_send, rs_recv, t_send, t_recv, l_send, l_recv):
    p = Place(n)
    side = p.side
    rows = x0.shape[0]
    wr = w0_hbm.shape[0]
    total_rows = dx_ref.shape[0]
    k0 = w0_hbm.shape[1]
    k1 = w1_hbm.shape[1]
    mine = pl.ds(pl.multiple_of(p.me * wr, wr), wr)

    loads = [
        pltpu.make_async_copy(w0_hbm, w0.at[mine, pl.ds(0, k0)], local_sems.at[0]),
        pltpu.make_async_copy(w1_hbm, w1.at[mine], local_sems.at[1]),
        pltpu.make_async_copy(w2_hbm, w2.at[mine], local_sems.at[2]),
        pltpu.make_async_copy(target_hbm, tbuf, local_sems.at[3]),
        pltpu.make_async_copy(acts_hbm.at[pl.ds(pl.multiple_of(p.me * rows, rows), rows)], x0, local_sems.at[4]),
    ]
    for load in loads:
        load.start()

    barrier = pltpu.get_barrier_semaphore()
    peers = [p.dev(way) for way in (XP, XM, YP, YM)] + [p.dev((0, 0), True)]
    for peer in peers:
        pl.semaphore_signal(barrier, inc=1, device_id={"model": peer}, device_id_type=MESH)

    lane = lax.broadcasted_iota(jnp.int32, (wr, LANES), 1)
    eye = (lax.broadcasted_iota(jnp.int32, (wr, wr), 0) == lax.broadcasted_iota(jnp.int32, (wr, wr), 1))
    uext = jnp.zeros((wr, LANES), F32)
    for i, ref in enumerate((u0_ref, u1_ref, u2_ref)):
        column = jnp.sum(jnp.where(eye, jnp.broadcast_to(ref[...], (wr, wr)), 0.0), axis=1, keepdims=True)
        uext = jnp.where(lane == i, column, uext)
    w0[mine, pl.ds(k0, LANES)] = uext.astype(BF16)

    pl.semaphore_wait(barrier, len(peers))

    def weight_at(ref):
        return lambda dev, s: ref.at[pl.ds(pl.multiple_of(dev * wr, wr), wr), pl.ds(s[0], s[1] - s[0])]

    q = k1 // 4
    wide = k0 + LANES
    gathers = []
    for i, (ref, cuts) in enumerate(((w0, (0, LANES, 3 * LANES, 4 * LANES, wide)), (w1, (0, q, 2 * q, 3 * q, k1)), (w2, (0, q, 2 * q, 3 * q, k1)))):
        gathers.append(Gather(Chan(p, w_send.at[i], w_recv.at[i]), weight_at(ref), cuts))
    ga, gb, gc = gathers
    for i, g in enumerate(gathers):
        loads[i].wait()
        g.step0()

    loads[3].wait()
    eye32 = eye.astype(BF16)
    cols = tbuf.shape[1]

    def turn(j, carry):
        piece = dot(eye32, tbuf[pl.ds(pl.multiple_of(j * rows, rows), rows), :], NT).astype(BF16)
        chip = j // CORES
        tmine[lax.rem(j, CORES), chip // side, lax.rem(chip, side)] = piece
        return carry

    lax.fori_loop(0, n, turn, 0)
    spread = Spread(Chan(p, t_send, t_recv), tmine, tstage, trelay, tmid, tfinal)
    spread.pair_send()
    ga.step1()
    gb.step1()
    spread.pair_take()
    gc.step1()
    spread.first_send()
    ga.step2()
    gb.step2()
    spread.first_relay()
    gc.step2()
    ga.step3()
    ga.step4()
    ga.finish()

    def matvec(vec, ref, dims, width):
        return dot(vec, ref[:, pl.ds(0, width)], dims)

    def power(i, w_ref, width, u16):
        for step in range(POWER_STEPS):
            pv = matvec(u16.astype(BF16), w_ref, NN, width)
            norm = jnp.sqrt(jnp.sum(pv * pv, axis=1, keepdims=True))
            v16 = (pv / jnp.maximum(norm, NORM_FLOOR)).astype(BF16)
            sv = matvec(v16, w_ref, NT, width)
            sigma = jnp.sqrt(jnp.sum(sv * sv, axis=1, keepdims=True))
            u16 = sv / sigma
        own = dot(v16, w_ref[mine, pl.ds(0, width)], NT) / sigma
        (un0_ref, un1_ref, un2_ref)[i][...] = own[0:1]
        (v0_ref, v1_ref, v2_ref)[i][...] = v16[0:1]
        return u16, v16, sigma[0:1, 0:1]

    def u_start(i):
        picked = (lax.broadcasted_iota(jnp.int32, (SUB, LANES), 1) == i).astype(BF16)
        return dot(picked, w0[:, pl.ds(k0, LANES)], NT)

    def forward(x_ref, w_ref, width, inv, y_ref, next_ref):
        def body(j, carry):
            at = pl.ds(pl.multiple_of(j * TILE, TILE), TILE)
            y = dot(x_ref[...], w_ref[at, pl.ds(0, width)], NT) * inv
            y_ref[:, at] = y
            if next_ref is not None:
                next_ref[:, at] = jnp.where(y >= 0, y, LEAK * y).astype(BF16)
            return carry

        lax.fori_loop(0, y_ref.shape[1] // TILE, body, 0)

    loads[4].wait()
    u16a, v16a, sa = power(0, w0, k0, u_start(0))
    inva = 1.0 / sa
    forward(x0, w0, k0, inva, y0, x1)
    gb.step3()
    gb.step4()
    spread.second_send()
    gc.step3()
    gb.finish()
    u16b, v16b, sb = power(1, w1, k1, u_start(1))
    invb = 1.0 / sb
    gc.step4()
    spread.second_relay()
    forward(x1, w1, k1, invb, y1, x2)
    gc.finish()
    u16c, v16c, sc = power(2, w2, k1, u_start(2))
    invc = 1.0 / sc
    forward(x2, w2, k1, invc, y2, None)
    spread.finish()

    lane1 = lax.broadcasted_iota(jnp.int32, (1, LANES), 1)
    sig_ref[...] = jnp.where(lane1 == 0, sa, jnp.where(lane1 == 1, sb, sc))

    scale = 1.0 / total_rows
    eyer = (lax.broadcasted_iota(jnp.int32, (rows, rows), 0) == lax.broadcasted_iota(jnp.int32, (rows, rows), 1)).astype(BF16)
    zero11 = jnp.zeros((1, 1), F32)

    def total(value):
        return jnp.sum(jnp.sum(value, axis=0, keepdims=True), axis=1, keepdims=True)

    loss = zero11
    corr = zero11
    span = TILE // (CORES * wr)
    for j in range(y2.shape[1] // TILE):
        at = pl.ds(j * TILE, TILE)
        block = tfinal[j * span // side] if span == side else None
        t = dot(eyer, block.reshape(TILE, rows), NT)
        residual = y2[:, at] - t
        g = residual * scale
        grad[:, at] = g
        low[:, at] = g.astype(BF16)
        loss = loss + total(residual * residual)
        corr = corr + total(g * y2[:, at])

    lossbuf[p.dev((0, 0)) // CORES] = jnp.broadcast_to(loss, lossbuf.shape[1:])
    lchan = Chan(p, l_send, l_recv)
    losspair[0] = jnp.broadcast_to(loss, losspair.shape[1:])
    lchan.start("pair", losspair.at[0], losspair.at[1], p.dev((0, 0), True))

    def share(x_ref, d_ref, width, corr, u16, v16):
        minus = [row_of(part[0:1], 1) for part in split3(u16[0:1] * (-corr))]
        sub = lax.broadcasted_iota(jnp.int32, (SUB, u16.shape[1]), 0)
        uu = jnp.zeros(sub.shape, F32)
        for i, part in enumerate(minus):
            uu = jnp.where(sub == i, jnp.broadcast_to(part.astype(F32), sub.shape), uu)
        sq[...] = uu.astype(BF16)

        def body(j, carry):
            at = pl.ds(pl.multiple_of(j * TILE, TILE), TILE)
            full = dot(low[:, at], x_ref[...], TN) + dot(sq[:, at], v16, TN)
            d_ref[j] = full.astype(BF16).reshape(side, CORES, wr, width)
            return carry

        lax.fori_loop(0, side, body, 0)

    def back(w_ref, width, inv, y_ref):
        corr = zero11
        for j in range(width // TILE):
            at = pl.ds(j * TILE, TILE)
            dx = (dot(low[...], w_ref[:, at], NN) * inv).astype(BF16)
            y = y_ref[:, at]
            g = dx.astype(F32) * jnp.where(y >= 0, 1.0, LEAK)
            grad[:, at] = g
            corr = corr + total(g * y)
        return corr

    def lower():
        low[...] = grad[...].astype(BF16)

    def reducer(i, blocks, mate, relay, main, relay2, main2, acc, width):
        return Reduce(Chan(p, rs_send.at[i], rs_recv.at[i]), blocks, mate, relay, main, relay2, main2, acc, width)

    rc = reducer(2, d2, m2, ra2, rb2, rc2, re2, rf2, k1)
    rb = reducer(1, d1, m1, ra1, rb1, rc1, re1, rf1, k1)
    ra = reducer(0, d0, m0, ra0, rb0, rc0, re0, rf0, k0)
    share(x2, d2, k1, corr, u16c, v16c)
    rc.pair_send()
    corr = back(w2, k1, invc, y1)
    lower()
    rc.pair_add()
    rc.far_send()
    share(x1, d1, k1, corr, u16b, v16b)
    rb.pair_send()
    corr = back(w1, k1, invb, y0)
    lower()
    rc.far_add()
    rb.pair_add()
    rb.far_send()

    out_rows = pl.ds(pl.multiple_of(p.me * rows, rows), rows)
    for j in range(k0 // TILE):
        at = pl.ds(j * TILE, TILE)
        dx_ref[out_rows, at] = (dot(low[...], w0[:, at], NN) * inva).astype(BF16)
    share(x0, d0, k0, corr, u16a, v16a)
    ra.pair_send()

    part = rows // DX_PARTS
    gd = []
    for i in range(DX_PARTS):
        def dx_at(dev, s, i=i):
            return dx_ref.at[pl.ds(pl.multiple_of(dev * rows + (i * part + s[0]), 16), s[1] - s[0])]

        gd.append(Gather(Chan(p, dx_send.at[i], dx_recv.at[i]), dx_at, [part * k // 4 for k in range(5)]))
    for g in gd:
        g.step0()

    lchan.wait("pair", losspair.at[1])
    here = p.dev((0, 0)) // CORES
    lossbuf[here] = losspair[0] + losspair[1]
    lg = Gather(lchan, lambda dev, s: lossbuf.at[dev // CORES], (0, 0, 1, 1, 1), pair=False)

    ra.pair_add()
    rc.near_add()
    rb.far_add()
    ra.far_send()
    lg.step0()
    gd[0].step1()
    rc.far2_add()
    rb.near_add()
    ra.far_add()
    lg.step1()
    gd[1].step1()
    rc.finish(g2_ref, invc)
    rb.far2_add()
    ra.near_add()
    lg.step2()
    gd[0].step2()
    rb.finish(g1_ref, invb)
    ra.far2_add()
    lg.step3()
    gd[1].step2()
    ra.finish(g0_ref, inva)
    lg.step4()
    gd[0].step3()
    gd[1].step3()
    gd[0].step4()
    gd[1].step4()
    whole = jnp.zeros(losspair.shape[1:], F32)
    for k in range(n // CORES):
        whole = whole + lossbuf[k]
    loss_ref[...] = whole[0:1, 0:1] * (0.5 * scale)
    gd[0].finish()
    gd[1].finish()
    for chan in [g.chan for g in gathers] + [spread.chan, lchan, ra.chan, rb.chan, rc.chan] + [g.chan for g in gd]:
        chan.drain()


def device_program(n, acts_in, w_first, w_middle, w_last, u_first, u_middle, u_last, target):
    side = math.isqrt(n // CORES)
    total_rows, k0 = acts_in.shape
    rows = total_rows // n
    wr, k1 = w_middle.shape
    width = wr * n
    tcols = target.shape[1]
    chips = side * side

    def reduce_bufs(k):
        q = k // 4
        return [pltpu.VMEM((2, 2, side, wr, q), BF16), pltpu.VMEM((2, 2, side, wr, 2 * q), BF16),
                pltpu.VMEM((2, 2, wr, q), BF16), pltpu.VMEM((2, 2, wr, 2 * q), BF16), pltpu.VMEM((2, wr, 2 * q), F32)]

    vmem = pl.BlockSpec(memory_space=pltpu.VMEM)
    anym = pl.BlockSpec(memory_space=pl.ANY)
    out_shape = (
        jax.ShapeDtypeStruct((1, 1), F32), jax.ShapeDtypeStruct((total_rows, k0), BF16),
        jax.ShapeDtypeStruct((wr, k0), F32), jax.ShapeDtypeStruct((wr, k1), F32), jax.ShapeDtypeStruct((wr, k1), F32),
        jax.ShapeDtypeStruct((1, wr), F32), jax.ShapeDtypeStruct((1, wr), F32), jax.ShapeDtypeStruct((1, wr), F32),
        jax.ShapeDtypeStruct((1, k0), BF16), jax.ShapeDtypeStruct((1, k1), BF16), jax.ShapeDtypeStruct((1, k1), BF16),
        jax.ShapeDtypeStruct((1, LANES), F32))
    scratch = [
        pltpu.VMEM((width, k0 + LANES), BF16), pltpu.VMEM((width, k1), BF16), pltpu.VMEM((width, k1), BF16),
        pltpu.VMEM((rows, k0), BF16), pltpu.VMEM((rows, k1), BF16), pltpu.VMEM((rows, k1), BF16),
        pltpu.VMEM((rows, width), F32), pltpu.VMEM((rows, width), F32), pltpu.VMEM((rows, width), F32),
        pltpu.VMEM((rows, width), F32), pltpu.VMEM((rows, width), BF16), pltpu.VMEM((SUB, width), BF16),
        pltpu.VMEM((total_rows, tcols), BF16),
        pltpu.VMEM((CORES, side, side, tcols, rows), BF16), pltpu.VMEM((CORES, side, side, tcols, rows), BF16),
        pltpu.VMEM((4, 2, side // 2, tcols, rows), BF16), pltpu.VMEM((2, side, side, tcols, rows), BF16),
        pltpu.VMEM((side, side, CORES, tcols, rows), BF16),
        pltpu.VMEM((chips, 8, LANES), F32), pltpu.VMEM((2, 8, LANES), F32),
        pltpu.VMEM((side, side, CORES, wr, k0), BF16), pltpu.VMEM((side, side, CORES, wr, k1), BF16), pltpu.VMEM((side, side, CORES, wr, k1), BF16),
        pltpu.VMEM((side, side, wr, k0), BF16), pltpu.VMEM((side, side, wr, k1), BF16), pltpu.VMEM((side, side, wr, k1), BF16),
        *reduce_bufs(k0), *reduce_bufs(k1), *reduce_bufs(k1),
        pltpu.SemaphoreType.DMA((5,)),
        pltpu.SemaphoreType.DMA((3, AG_SEMS)), pltpu.SemaphoreType.DMA((3, AG_SEMS)),
        pltpu.SemaphoreType.DMA((DX_PARTS, AG_SEMS)), pltpu.SemaphoreType.DMA((DX_PARTS, AG_SEMS)),
        pltpu.SemaphoreType.DMA((3, RS_SEMS)), pltpu.SemaphoreType.DMA((3, RS_SEMS)),
        pltpu.SemaphoreType.DMA((TG_SEMS,)), pltpu.SemaphoreType.DMA((TG_SEMS,)),
        pltpu.SemaphoreType.DMA((AG_SEMS,)), pltpu.SemaphoreType.DMA((AG_SEMS,)),
    ]
    import functools
    outs = pl.pallas_call(
        functools.partial(kernel, n),
        out_shape=out_shape,
        in_specs=[anym, anym, anym, anym, vmem, vmem, vmem, anym],
        out_specs=(vmem,) * len(out_shape),
        scratch_shapes=scratch,
        compiler_params=pltpu.CompilerParams(collective_id=0, has_side_effects=True, vmem_limit_bytes=50 * 1024 * 1024),
        name="stack",
    )(acts_in, w_first, w_middle, w_last, u_first.reshape(1, wr), u_middle.reshape(1, wr), u_last.reshape(1, wr), target)
    loss, dx, g0, g1, g2, un0, un1, un2, v0, v1, v2, sig = outs
    return (loss.reshape(1), dx, g0, g1, g2, un0.reshape(wr), un1.reshape(wr), un2.reshape(wr),
            v0.reshape(k0), v1.reshape(k1), v2.reshape(k1), sig[0, :3])


def solution(mesh):
    n = mesh.shape["model"]
    row_spec = P("rep", None)
    weight_spec = P(("rep", "model"), None)
    vector_spec = P(("rep", "model"))
    group_spec = P("rep")
    in_specs = (row_spec, weight_spec, weight_spec, weight_spec, vector_spec, vector_spec, vector_spec, P("rep", "model"))
    out_specs = (group_spec, row_spec, weight_spec, weight_spec, weight_spec, vector_spec, vector_spec, vector_spec, group_spec, group_spec, group_spec, group_spec)
    return jax.shard_map(lambda *args: device_program(n, *args), mesh=mesh, in_specs=in_specs, out_specs=out_specs, check_vma=False)
```

time: 735 us -> 129 us (0.18)
  waiting for transfers between devices: 373 us -> 0 us
  blocking collectives: 229 us -> 0 us
  Pallas kernels: 0 us -> 107 us
  matrix products: 91.5 us -> 0 us
  between operations: 24.1 us -> 2.38 us
  local copies, waits for them, and re-layouts: 8.41 us -> 17.6 us
    psum x5 -> x0, blocking collectives: 229 us -> none  [the longest x2 93.8 us: power_steps(): lax.psum(jnp.dot(u_vec.astype(jnp.bfloat16), w_local, preferred_element_t...]
    reduce_scatter x2 -> x0, waiting for transfers between devices: 212 us -> none  [device_program(): lax.psum_scatter(share_in, 'model', scatter_dimension=1, tiled=True)]
    all_gather x2 -> x0, waiting for transfers between devices: 131 us -> none  [device_program(): layer_in.append(lax.all_gather(act_local, 'model', axis=1, tiled=True))]
    pallas_call x0 -> x1, Pallas kernels: none -> 107 us  [device_program(): pl.pallas_call(functools.partial(kernel, n), out_shape=out_shape, in_spec...]
    dot_general x21 -> x0, matrix products: 91.5 us -> none  [the longest x3 30.5 us: device_program(): lax.dot_general(grad_low, layer_in[layer], BATCH_DIMS, preferred_element_...]
    psum x1 -> x0, waiting for transfers between devices: 29.3 us -> none  [device_program(): grad_in = lax.psum(share_in, 'model')]
    unnamed x29 -> x20, local copies, waits for them, and re-layouts: 8.38 us -> 17.1 us
  transfers between devices with their start and end apart: 5 -> 0, of which waited for: 5 -> 0; matrix products, arithmetic and copies ran while one was open for 5% -> 0% of each run, Pallas kernels for 0% -> 0%
where the time goes in v2:
time: 129 us
  Pallas kernels  107 us (83%)
  local copies, waits for them, and re-layouts  17.6 us (14%)
  between operations  2.38 us (2%)
  other arithmetic  1.78 us (1%)
    pallas_call x1, Pallas kernels, device_program(): pl.pallas_call(functools.partial(kernel, n), out_shape=out_shape, in_spec...  107 us
    unnamed x20, local copies, waits for them, and re-layouts  17.1 us

profile of v2, /device:TPU:97, one launch (start us, length us, event | category | flops | bytes accessed | tf_op | source)
XLA Modules:
  0.0 129.0 jit_solution(17310122873482878658)
XLA Ops:
  0.6 1.9 %copy.20.target_hbm = bf16[8192,32]{1,0:T(8,128)(2,1)S(1)} copy(bf16[8192,32]{0,1:T(8,128)(2,1)} %param.15) | data formatting | bytes 1048576 | tf_op args[7]
  2.6 0.0 copy-start
  2.6 0.8 copy-done
  3.4 0.0 copy-start.1
  3.4 0.8 copy-done.1
  4.3 0.0 copy-start.2
  4.3 0.8 copy-done.2
  5.0 0.0 copy-start.3
  5.0 0.7 copy-done.3
  5.7 0.0 copy-start.4
  5.7 0.7 copy-done.4
  6.3 0.0 copy-start.5
  6.3 0.7 copy-done.5
  7.0 107.3 %stack.1 = (f32[1,1]{1,0:T(1,128)}, bf16[8192,512]{1,0:T(8,128)(2,1)}, f32[32,512]{1,0:T(8,128)S(1)}, f32[32,1024]{1,0:T(8,128)S(1)}, f32[32,1024]{1,0:T(8,128)S...) custom-call(bf16[8192,512]{1,0:T(8,128)(2,1)} %acts_hbm.1, ...), custom_call_target="tpu_custom_call" | custom-call | tf_op jit(solution)/shard_map/stack/pallas_call | solution.py:675
  114.3 0.5 slice_bitcast_fusion
  114.8 0.6 reduce
  115.3 0.6 reduce.1
  115.9 0.6 reduce.2
  117.1 7.3 %copy.30 = bf16[8192,512]{1,0:T(8,128)(2,1)} copy(bf16[8192,512]{1,0:T(8,128)(2,1)} %get-tuple-element.49) | data formatting | bytes 16777216
  124.4 0.6 copy.31
  125.1 0.7 copy.32
  125.7 0.7 copy.33
  126.4 0.5 copy.34
  126.9 0.5 copy.35
  127.4 0.5 copy.36
Async XLA Ops:
  2.6 0.8 copy-start
  3.4 0.8 copy-start.1
  4.3 0.8 copy-start.2
  5.0 0.7 copy-start.3
  5.7 0.7 copy-start.4
  6.3 0.7 copy-start.5

commit v3 on v0

v3 whole, which is shorter than its diff:
```python
import functools
import math

import jax
import jax.numpy as jnp
from jax import lax
from jax.experimental import pallas as pl
from jax.experimental.pallas import tpu as pltpu
from jax.sharding import PartitionSpec as P

LEAK = 0.2
NORM_FLOOR = 1e-12
POWER_STEPS = 2
MESH = pl.DeviceIdType.MESH
F32 = jnp.float32
BF16 = jnp.bfloat16
NN = (((1,), (0,)), ((), ()))
NT = (((1,), (1,)), ((), ()))
CORES = 2
LANES = 128
SUB = 16
TILE = 256
FTILE = 512
VMEM_LIMIT = 40 * 1024 * 1024
TAKE_LIMIT = 66338816
EMIT_LIMIT = 12 * 1024 * 1024
DX_PARTS = 2
XP, XM, YP, YM = (1, 0), (-1, 0), (0, 1), (0, -1)


def dot(lhs, rhs, dims):
    return lax.dot_general(lhs, rhs, dims, preferred_element_type=F32)


class Place:
    def __init__(self, n):
        self.side = math.isqrt(n // CORES)
        me = lax.axis_index("model")
        self.me = me
        self.core = lax.rem(me, CORES)
        self.x = lax.rem(me // CORES, self.side)
        self.y = me // (CORES * self.side)

    def col(self, dx):
        return lax.rem(self.x + (dx + self.side), self.side)

    def row(self, dy):
        return lax.rem(self.y + (dy + self.side), self.side)

    def dev(self, rel, other=False):
        core = 1 - self.core if other else self.core
        return (self.row(rel[1]) * self.side + self.col(rel[0])) * CORES + core

    def at(self, x, y):
        return (y * self.side + x) * CORES + self.core

    def norm(self, rel):
        s = self.side
        half = s // 2
        return tuple((r + half - 1) % s - (half - 1) for r in rel)


class Link:
    def __init__(self, place, send_sem, recv_sems):
        self.place, self.send_sem, self.recv_sems = place, send_sem, recv_sems

    def copy(self, i, src, dst, target, send_sem=None):
        return pltpu.make_async_remote_copy(
            src_ref=src, dst_ref=dst, send_sem=self.send_sem if send_sem is None else send_sem,
            recv_sem=self.recv_sems.at[i], device_id={"model": target}, device_id_type=MESH)

    def start(self, i, src, dst, target, send_sem=None):
        self.copy(i, src, dst, target, send_sem).start()

    def wait(self, i, dst):
        self.copy(i, dst, dst, self.place.dev((0, 0), True)).wait_recv()

    def drain(self, sent, send_sem=None):
        self.copy(0, sent, sent, self.place.dev((0, 0), True), send_sem).wait_send()


class Gather:
    def __init__(self, link, ref_at, bulk, cuts):
        self.link, self.ref_at, self.bulk, self.place = link, ref_at, bulk, link.place
        a, b, c, d, e = cuts
        self.full, self.mid, self.outer = ((a, e),), ((b, d),), ((a, b), (d, e))
        self.half = {"x": ((a, c),), "y": ((c, e),)}
        self.fwd = {"x": ((b, c),), "y": ((c, d),)}
        self.bwd = {"x": ((a, b),), "y": ((d, e),)}

    def number(self, rel):
        return (rel[1] + 1) * self.place.side + rel[0] + 1

    def start(self, rel, spans, way, src=None):
        there = self.number(self.place.norm((rel[0] - way[0], rel[1] - way[1])))
        for s in spans:
            ref = self.ref_at(self.place.dev(rel), s)
            self.link.start(there, ref if src is None else src, ref, self.place.dev(way))

    def take(self, rel):
        self.link.wait(self.number(rel), self.ref_at(self.place.dev(rel), self.full[0]))

    def mate(self, rel, src=None):
        ref = self.ref_at(self.place.dev(rel), self.full[0])
        self.link.start(self.number((0, 0)), ref if src is None else src, ref, self.place.dev((0, 0), True))

    def cross(self, rel, axis):
        for way in ((YP, YM) if axis == "x" else (XP, XM)):
            self.start(rel, self.half[axis], way)

    def relay(self, rel, axis, first):
        off = rel[0] if axis == "x" else rel[1]
        way = {("x", -1): XP, ("x", 1): XM, ("y", -1): YP, ("y", 1): YM}[(axis, off)]
        self.start(rel, (self.fwd if off < 0 else self.bwd)[first], way)

    def step0(self, src=None):
        for way in (XP, YP, XM, YM):
            self.start((0, 0), self.full, way, src)
        self.mate((0, 0), src)

    def step1(self):
        for way in (XP, YP, XM, YM):
            rel = (-way[0], -way[1])
            self.take(rel)
            self.start(rel, self.mid if way in (XP, YP) else self.outer, way)
            self.cross(rel, "x" if way[0] else "y")
            self.mate(rel)

    def step2(self):
        for rel, axis in (((2, 0), "x"), ((0, 2), "y")):
            self.take(rel)
            self.cross(rel, axis)
            self.mate(rel)
        for rel in ((-1, -1), (-1, 1), (1, -1), (1, 1)):
            self.take(rel)
            self.relay(rel, "y", "x")
            self.relay(rel, "x", "y")
            self.mate(rel)

    def step3(self):
        for d in (-1, 1):
            self.take((2, d))
            self.relay((2, d), "y", "x")
            self.mate((2, d))
            self.take((d, 2))
            self.relay((d, 2), "x", "y")
            self.mate((d, 2))

    def step4(self):
        self.take((2, 2))
        self.mate((2, 2))

    def finish(self):
        self.link.wait(self.number((0, 0)), self.bulk(self.place.side ** 2))

    def drain(self):
        self.link.drain(self.bulk(CORES * self.place.side ** 2 - 1))


class Reduce:
    def __init__(self, link, blocks, mate, relay, main, relay2, main2, acc, width):
        self.link, self.place = link, link.place
        self.blocks, self.mate = blocks, mate
        self.relay, self.main, self.relay2, self.main2, self.acc = relay, main, relay2, main2, acc
        q = width // 4
        self.q = q
        self.cols = {"x": ((q, 2 * q), (0, q), (0, 2 * q)), "y": ((2 * q, 3 * q), (3 * q, 4 * q), (2 * q, 4 * q))}

    def at(self, axis, pos, span):
        cols = pl.ds(span[0], span[1] - span[0])
        if axis == "x":
            return self.blocks.at[:, pos, self.place.core, :, cols]
        return self.blocks.at[pos, :, self.place.core, :, cols]

    def one(self, dx, dy, span):
        return self.blocks.at[self.place.row(dy), self.place.col(dx), self.place.core, :, pl.ds(span[0], span[1] - span[0])]

    def pair_send(self):
        p = self.place
        self.link.start(0, self.blocks.at[:, :, 1 - p.core], self.mate, p.dev((0, 0), True))

    def pair_add(self):
        p = self.place
        self.link.wait(0, self.mate)
        for k in range(p.side):
            mine = self.blocks.at[k, :, p.core]
            mine[...] = (mine[...].astype(F32) + self.mate[k].astype(F32)).astype(BF16)

    def pos(self, axis, d):
        return self.place.col(d) if axis == "x" else self.place.row(d)

    def ways(self, axis):
        return (XP, XM) if axis == "x" else (YP, YM)

    def far_send(self):
        for h, axis in enumerate(("x", "y")):
            for s, way in enumerate(self.ways(axis)):
                self.link.start(1 + 2 * h + s, self.at(axis, self.pos(axis, 2), self.cols[axis][s]),
                                self.relay.at[h, s], self.place.dev(way))

    def far_add(self):
        for h, axis in enumerate(("x", "y")):
            for s, way in enumerate(self.ways(axis)):
                self.link.wait(1 + 2 * h + s, self.relay.at[h, s])
                step = 1 if s == 0 else -1
                ref = self.at(axis, self.pos(axis, step), self.cols[axis][s])
                ref[...] = (ref[...].astype(F32) + self.relay[h, s].astype(F32)).astype(BF16)
                self.link.start(5 + h, self.at(axis, self.pos(axis, step), self.cols[axis][2]),
                                self.main.at[h, s], self.place.dev(way))

    def near_add(self):
        p = self.place
        for h, (axis, cross) in enumerate((("x", "y"), ("y", "x"))):
            self.link.wait(5 + h, self.main.at[h])
            own = self.pos(cross, 0)
            span = self.cols[axis][2]
            self.acc[h] = (self.one(0, 0, span)[...].astype(F32) + self.main[h, 0, own].astype(F32)
                           + self.main[h, 1, own].astype(F32))
            ref = self.at(axis, self.pos(axis, 0), span)
            ref[...] = (ref[...].astype(F32) + self.main[h, 0].astype(F32) + self.main[h, 1].astype(F32)).astype(BF16)
            for s, way in enumerate(self.ways(cross)):
                d = (0, 2) if cross == "y" else (2, 0)
                self.link.start(7 + 2 * h + s, self.one(d[0], d[1], self.cols[axis][s]),
                                self.relay2.at[h, s], p.dev(way))

    def far2_add(self):
        p = self.place
        for h, (axis, cross) in enumerate((("x", "y"), ("y", "x"))):
            for s, way in enumerate(self.ways(cross)):
                self.link.wait(7 + 2 * h + s, self.relay2.at[h, s])
                ref = self.one(way[0], way[1], self.cols[axis][s])
                ref[...] = (ref[...].astype(F32) + self.relay2[h, s].astype(F32)).astype(BF16)
                self.link.start(11 + h, self.one(way[0], way[1], self.cols[axis][2]),
                                self.main2.at[h, s], p.dev(way))

    def finish(self, out_ref, inv):
        for h in range(2):
            self.link.wait(11 + h, self.main2.at[h])
            out_ref[:, pl.ds(2 * self.q * h, 2 * self.q)] = (
                self.acc[h] + self.main2[h, 0].astype(F32) + self.main2[h, 1].astype(F32)) * inv


class Spread:
    def __init__(self, link, send_sems, mine, stage, relay, mid, final):
        self.link, self.place, self.sems = link, link.place, send_sems
        self.mine, self.stage, self.relay, self.mid, self.final = mine, stage, relay, mid, final

    def pair_send(self):
        p = self.place
        self.link.start(0, self.mine.at[1 - p.core], self.stage.at[p.core], p.dev((0, 0), True), self.sems[0])

    def pair_take(self):
        p = self.place
        self.stage[p.core] = self.mine[p.core]
        self.link.wait(0, self.stage.at[1 - p.core])

    def src(self, h, pos, lo, hi):
        rest = pl.ds(lo, hi - lo)
        return self.stage.at[h, rest, pos] if h == 0 else self.stage.at[h, pos, rest]

    def first_send(self):
        p = self.place
        s2 = p.side // 2
        for h in range(2):
            here = p.x if h == 0 else p.y
            ways = (XP, XM) if h == 0 else (YP, YM)
            pos = p.col if h == 0 else p.row
            for s, way in enumerate(ways):
                self.link.start(1 + 2 * h + s, self.src(h, pos(2), s * s2, s * s2 + s2), self.relay.at[h, s], p.dev(way), self.sems[1])
            for s, way in enumerate(ways):
                d = 1 if s == 0 else -1
                self.link.start(5 + h, self.src(h, pos(d), 0, p.side), self.mid.at[h, here], p.dev(way), self.sems[1])
            self.mid[h, here] = self.src(h, here, 0, p.side)[...]

    def first_relay(self):
        p = self.place
        s2 = p.side // 2
        for h in range(2):
            ways = (XP, XM) if h == 0 else (YP, YM)
            pos = p.col if h == 0 else p.row
            for s, way in enumerate(ways):
                self.link.wait(1 + 2 * h + s, self.relay.at[h, s])
                self.link.start(5 + h, self.relay.at[h, s],
                                self.mid.at[h, pos(-1 if s == 0 else 1), pl.ds(s * s2, s2)], p.dev(way), self.sems[1])

    def second_send(self):
        p = self.place
        s2 = p.side // 2
        for h in range(2):
            self.link.wait(5 + h, self.mid.at[h, 0:p.side - 1])
            cross = p.row if h == 0 else p.col
            ways = (YP, YM) if h == 0 else (XP, XM)
            for s, way in enumerate(ways):
                self.link.start(7 + 2 * h + s, self.mid.at[h, pl.ds(s * s2, s2), cross(2)],
                                self.relay.at[2 + h, s], p.dev(way), self.sems[2])
            for s, way in enumerate(ways):
                self.link.start(11, self.mid.at[h, :, cross(1 if s == 0 else -1)],
                                self.dst(h, cross(0), 0, p.side), p.dev(way), self.sems[2])
            self.dst(h, cross(0), 0, p.side)[...] = self.mid[h, :, cross(0)]

    def dst(self, h, pos, lo, hi):
        rest = pl.ds(lo, hi - lo)
        return self.final.at[pos, rest, h] if h == 0 else self.final.at[rest, pos, h]

    def second_relay(self):
        p = self.place
        s2 = p.side // 2
        for h in range(2):
            cross = p.row if h == 0 else p.col
            ways = (YP, YM) if h == 0 else (XP, XM)
            for s, way in enumerate(ways):
                self.link.wait(7 + 2 * h + s, self.relay.at[2 + h, s])
                self.link.start(11, self.relay.at[2 + h, s],
                                self.dst(h, cross(-1 if s == 0 else 1), s * s2, s * s2 + s2), p.dev(way), self.sems[2])

    def finish(self):
        self.link.wait(11, self.mid.at[:, 0:self.place.side - 1])

    def drain(self):
        self.link.drain(self.mine.at[0], self.sems[0])
        self.link.drain(self.mid, self.sems[1])
        self.link.drain(self.mid, self.sems[2])


class Total:
    def __init__(self, link, sent, got):
        self.link, self.place, self.sent, self.got = link, link.place, sent, got
        p = self.place
        odd = lambda c: c + 1 - 2 * lax.rem(c, 2)
        self.targets = [p.dev((0, 0), True), p.at(odd(p.x), p.y), p.at(p.side - 1 - p.x, p.y), p.at(p.x, odd(p.y)), p.at(p.x, p.side - 1 - p.y)]

    def send(self, i):
        self.link.start(i, self.sent.at[i], self.got.at[i], self.targets[i])

    def first(self, value):
        self.sent[0] = jnp.broadcast_to(value, self.sent.shape[1:])
        self.send(0)

    def step(self, i):
        self.link.wait(i, self.got.at[i])
        value = self.sent[i] + self.got[i]
        if i + 1 < len(self.targets):
            self.sent[i + 1] = value
            self.send(i + 1)
        return value

    def drain(self):
        self.link.drain(self.sent)


def split3(value):
    hi = value.astype(BF16)
    rest = value - hi.astype(F32)
    mid = rest.astype(BF16)
    lo = (rest - mid.astype(F32)).astype(BF16)
    return hi, mid, lo


def kernel(n, acts_hbm, wcat, tmine,
           loss_ref, dx_ref, g0_ref, g1_ref, g2_ref, un0_ref, un1_ref, un2_ref, v0_ref, v1_ref, v2_ref, sig_ref,
           wa, wb, x0, x1, x2, xt0, xt1, xt2, yt0, yt1, yt2, mt, mask0, mask1, lowt, low, low2, dxa, dxb, uc, sq, vbuf,
           tstage, trelay, tmid, tfinal, losssent, lossgot,
           d0, d1, d2, m0, m1, m2,
           ra0, rb0, rc0, re0, rf0, ra1, rb1, rc1, re1, rf1, ra2, rb2, rc2, re2, rf2,
           acts_sem, send_sems, w_recv, dx_recv, rs_recv, t_recv, l_recv):
    p = Place(n)
    side = p.side
    rows = x0.shape[0]
    wr = wcat.shape[0]
    total_rows, k0 = dx_ref.shape
    k1 = wb.shape[1]
    wide = k0 + LANES
    width = wa.shape[0]
    mine = pl.ds(pl.multiple_of(p.me * wr, wr), wr)
    w0 = wa.at[:, pl.ds(0, k0)]
    ucols = wa.at[:, pl.ds(k0, LANES)]
    w1 = wa.at[:, pl.ds(wide, k1)]
    w2 = wb

    acts_load = pltpu.make_async_copy(acts_hbm.at[pl.ds(pl.multiple_of(p.me * rows, rows), rows)], x0, acts_sem)
    acts_load.start()

    barrier = pltpu.get_barrier_semaphore()
    peers = [p.dev(way) for way in (XP, XM, YP, YM)] + [p.dev((0, 0), True)]
    for peer in peers:
        pl.semaphore_signal(barrier, inc=1, device_id={"model": peer}, device_id_type=MESH)
    pl.semaphore_wait(barrier, len(peers))

    def gather_weight(i, ref):
        def ref_at(dev, s):
            return ref.at[pl.ds(pl.multiple_of(dev * wr, wr), wr), pl.ds(s[0], s[1] - s[0])]

        tiles = ref.shape[1] // LANES
        cuts = [LANES * ((tiles * k) // 4) for k in range(5)]
        return Gather(Link(p, send_sems.at[i], w_recv.at[i]), ref_at, lambda k: ref.at[pl.ds(0, k * wr)], cuts)

    ga, gb = gather_weight(0, wa), gather_weight(1, wb)
    for g, ref, lo in ((ga, wa, 0), (gb, wb, wa.shape[1])):
        own = wcat.at[:, pl.ds(lo, ref.shape[1])]
        g.step0(own)
        ref[mine] = own[...]

    spread = Spread(Link(p, send_sems.at[2], t_recv), [send_sems.at[k] for k in (2, 3, 4)], tmine, tstage, trelay, tmid, tfinal)
    spread.pair_send()
    eye_big = (lax.broadcasted_iota(jnp.int32, (TILE, TILE), 0) == lax.broadcasted_iota(jnp.int32, (TILE, TILE), 1)).astype(BF16)
    eye_small = eye_big[0:SUB, 0:SUB]

    def turn(src, dst):
        for j in range(max(src.shape) // TILE):
            at = pl.ds(j * TILE, TILE)
            if src.shape[0] > TILE:
                dst[:, at] = dot(eye_big, src[at, :], NT).astype(BF16)
            else:
                dst[at, :] = dot(eye_big, src[:, at], NT).astype(BF16)

    def power(i, w_ref):
        picked = (lax.broadcasted_iota(jnp.int32, (SUB, LANES), 1) == i).astype(BF16)
        u_row = dot(picked, ucols[...], NT).astype(BF16)
        for step in range(POWER_STEPS):
            pv = dot(u_row, w_ref[...], NN)
            norm = jnp.sqrt(jnp.sum(pv * pv, axis=1, keepdims=True))
            v16 = (pv / jnp.maximum(norm, NORM_FLOOR)).astype(BF16)
            sv = dot(w_ref[...], v16, NT)
            sigma = jnp.sqrt(jnp.sum(sv * sv, axis=0, keepdims=True))
            ucol = sv / sigma
            if step + 1 < POWER_STEPS:
                u_row = dot(eye_small, ucol.astype(BF16), NT).astype(BF16)
        uc[i] = ucol
        vbuf[i, :, pl.ds(0, v16.shape[1])] = v16
        sigma = sigma[0:1, 0:1]
        own = dot(v16, w_ref[mine, :], NT) / sigma
        (un0_ref, un1_ref, un2_ref)[i][...] = own[0:1]
        (v0_ref, v1_ref, v2_ref)[i][...] = v16[0:1]
        return sigma

    def forward(w_ref, xt_ref, inv, y_ref, next_ref, mask_ref):
        for j in range(width // FTILE):
            at = pl.ds(j * FTILE, FTILE)
            y = dot(w_ref[at, :], xt_ref[...], NN) * inv
            y_ref[at, :] = y
            if next_ref is not None:
                next_ref[at, :] = jnp.where(y >= 0, y, LEAK * y).astype(BF16)
                mask_ref[at, :] = jnp.where(y >= 0, 1.0, 0.0).astype(BF16)

    acts_load.wait()
    turn(x0, xt0)
    ga.step1()
    gb.step1()
    spread.pair_take()
    ga.step2()
    gb.step2()
    spread.first_send()
    ga.step3()
    gb.step3()
    ga.step4()
    spread.first_relay()
    ga.finish()
    sa = power(0, w0)
    inva = 1.0 / sa
    spread.second_send()
    gb.step4()
    forward(w0, xt0, inva, yt0, xt1, mt)
    turn(xt1, x1)
    turn(mt, mask0)
    sb = power(1, w1)
    spread.second_relay()
    invb = 1.0 / sb
    forward(w1, xt1, invb, yt1, xt2, mt)
    gb.finish()
    sc = power(2, w2)
    invc = 1.0 / sc
    forward(w2, xt2, invc, yt2, None, None)
    turn(xt2, x2)
    turn(mt, mask1)
    spread.finish()

    lane1 = lax.broadcasted_iota(jnp.int32, (1, LANES), 1)
    sig_ref[...] = jnp.where(lane1 == 0, sa, jnp.where(lane1 == 1, sb, sc))

    scale = 1.0 / total_rows
    zero_row = jnp.zeros((1, rows), F32)

    def down(value):
        return jnp.sum(value, axis=0, keepdims=True)

    loss = zero_row
    corr = zero_row
    for j in range(side):
        at = pl.ds(j * TILE, TILE)
        y = yt2[at, :]
        residual = y - tfinal[j].reshape(TILE, rows).astype(F32)
        g = residual * scale
        lowt[at, :] = g.astype(BF16)
        loss = loss + down(residual * residual)
        corr = corr + down(g * y)
    whole = Total(Link(p, send_sems.at[10], l_recv), losssent, lossgot)
    whole.first(jnp.sum(loss, axis=1, keepdims=True))

    def share(i, x_ref, d_ref, corr):
        corr = jnp.sum(corr, axis=1, keepdims=True)
        parts = split3(uc[i] * (-corr))
        lane = lax.broadcasted_iota(jnp.int32, (width, SUB), 1)
        uu = jnp.zeros((width, SUB), F32)
        for k, part in enumerate(parts):
            uu = jnp.where(lane == k, part.astype(F32), uu)
        sq[...] = uu.astype(BF16)

        def body(j, carry):
            at = pl.ds(pl.multiple_of(j * TILE, TILE), TILE)
            full = dot(lowt[...], x_ref[:, at], NN) + dot(sq[...], vbuf[i, :, at], NN)
            d_ref[:, :, :, :, at] = full.astype(BF16).reshape(side, side, CORES, wr, TILE)
            return carry

        lax.fori_loop(0, x_ref.shape[1] // TILE, body, 0)

    def back(w_ref, inv, low_ref, out_ref, mask_ref, next_ref):
        for j in range(w_ref.shape[1] // TILE):
            at = pl.ds(j * TILE, TILE)
            dx = (dot(low_ref[...], w_ref[:, at], NN) * inv).astype(BF16)
            out_ref[:, at] = dx
            if mask_ref is not None:
                next_ref[:, at] = jnp.where(mask_ref[:, at].astype(F32) > 0.5, dx.astype(F32), LEAK * dx.astype(F32)).astype(BF16)

    def columns(dx_ref, yt_ref):
        corr = zero_row
        for j in range(width // TILE):
            at = pl.ds(j * TILE, TILE)
            y = yt_ref[at, :]
            g = dot(eye_big, dx_ref[:, at], NT) * jnp.where(y >= 0, 1.0, LEAK)
            lowt[at, :] = g.astype(BF16)
            corr = corr + down(g * y)
        return corr

    def reducer(i, blocks, mate, relay, main, relay2, main2, acc, cols):
        return Reduce(Link(p, send_sems.at[5 + i], rs_recv.at[i]), blocks, mate, relay, main, relay2, main2, acc, cols)

    rc = reducer(2, d2, m2, ra2, rb2, rc2, re2, rf2, k1)
    rb = reducer(1, d1, m1, ra1, rb1, rc1, re1, rf1, k1)
    ra = reducer(0, d0, m0, ra0, rb0, rc0, re0, rf0, k0)
    out_rows = pl.ds(pl.multiple_of(p.me * rows, rows), rows)
    turn(lowt, low)
    back(w2, invc, low, dxa, mask1, low2)
    back(w1, invb, low2, dxb, mask0, low)
    back(w0, inva, low, dx_ref.at[out_rows], None, None)

    part = rows // DX_PARTS
    gd = []
    for i in range(DX_PARTS):
        def dx_at(dev, s, i=i):
            return dx_ref.at[pl.ds(pl.multiple_of(dev * rows + (i * part + s[0]), SUB), s[1] - s[0])]

        gd.append(Gather(Link(p, send_sems.at[8 + i], dx_recv.at[i]), dx_at, lambda k: dx_ref.at[pl.ds(0, k * part)], [part * k // 4 for k in range(5)]))
    for g in gd:
        g.step0()
    share(2, x2, d2, corr)
    rc.pair_send()
    corr = columns(dxa, yt1)
    share(1, x1, d1, corr)
    rb.pair_send()
    rc.pair_add()
    rc.far_send()
    whole.step(0)
    corr = columns(dxb, yt0)
    share(0, x0, d0, corr)
    ra.pair_send()
    rb.pair_add()
    rb.far_send()
    gd[0].step1()
    ra.pair_add()
    ra.far_send()
    whole.step(1)
    rc.far_add()
    gd[1].step1()
    rb.far_add()
    ra.far_add()
    whole.step(2)
    rc.near_add()
    rb.near_add()
    ra.near_add()
    whole.step(3)
    gd[0].step2()
    rc.far2_add()
    rb.far2_add()
    ra.far2_add()
    loss_ref[...] = whole.step(4)[0:1, 0:1] * (0.5 * scale)
    gd[1].step2()
    rc.finish(g2_ref, invc)
    rb.finish(g1_ref, invb)
    ra.finish(g0_ref, inva)
    gd[0].step3()
    gd[1].step3()
    gd[0].step4()
    gd[1].step4()
    for g in gd:
        g.finish()
    ga.drain()
    gb.drain()
    spread.drain()
    whole.drain()
    ra.link.drain(dx_ref.at[pl.ds(0, (n - 1) * wr)])
    rb.link.drain(wb.at[pl.ds(0, (n - 1) * wr)])
    rc.link.drain(wb.at[pl.ds(0, (n - 1) * wr)])
    for g in gd:
        g.drain()


def device_program(n, acts_in, w_first, w_middle, w_last, u_first, u_middle, u_last, target):
    side = math.isqrt(n // CORES)
    total_rows, k0 = acts_in.shape
    rows = total_rows // n
    wr, k1 = w_middle.shape
    width = wr * n
    tcols = target.shape[1]
    hbm = pl.BlockSpec(memory_space=pltpu.HBM)
    chips = side * side

    def reduce_bufs(k):
        q = k // 4
        return [pltpu.VMEM((2, 2, side, wr, q), BF16), pltpu.VMEM((2, 2, side, wr, 2 * q), BF16),
                pltpu.VMEM((2, 2, wr, q), BF16), pltpu.VMEM((2, 2, wr, 2 * q), BF16), pltpu.VMEM((2, wr, 2 * q), F32)]

    vmem = pl.BlockSpec(memory_space=pltpu.VMEM)
    out_shape = (
        jax.ShapeDtypeStruct((1, 1), F32), jax.ShapeDtypeStruct((total_rows, k0), BF16),
        jax.ShapeDtypeStruct((wr, k0), F32), jax.ShapeDtypeStruct((wr, k1), F32), jax.ShapeDtypeStruct((wr, k1), F32),
        jax.ShapeDtypeStruct((1, wr), F32), jax.ShapeDtypeStruct((1, wr), F32), jax.ShapeDtypeStruct((1, wr), F32),
        jax.ShapeDtypeStruct((1, k0), BF16), jax.ShapeDtypeStruct((1, k1), BF16), jax.ShapeDtypeStruct((1, k1), BF16),
        jax.ShapeDtypeStruct((1, LANES), F32))
    scratch = [
        pltpu.VMEM((width, k0 + LANES + k1), BF16), pltpu.VMEM((width, k1), BF16),
        pltpu.VMEM((rows, k0), BF16), pltpu.VMEM((rows, k1), BF16), pltpu.VMEM((rows, k1), BF16),
        pltpu.VMEM((k0, rows), BF16), pltpu.VMEM((k1, rows), BF16), pltpu.VMEM((k1, rows), BF16),
        pltpu.VMEM((width, rows), F32), pltpu.VMEM((width, rows), F32), pltpu.VMEM((width, rows), F32),
        pltpu.VMEM((width, rows), BF16), pltpu.VMEM((rows, width), BF16), pltpu.VMEM((rows, width), BF16),
        pltpu.VMEM((width, rows), BF16), pltpu.VMEM((rows, width), BF16), pltpu.VMEM((rows, width), BF16),
        pltpu.VMEM((rows, width), BF16), pltpu.VMEM((rows, width), BF16),
        pltpu.VMEM((3, width, SUB), F32), pltpu.VMEM((width, SUB), BF16), pltpu.VMEM((3, SUB, k1), BF16),
        pltpu.VMEM((CORES, side, side, tcols, rows), BF16),
        pltpu.VMEM((4, 2, side // 2, tcols, rows), BF16), pltpu.VMEM((2, side, side, tcols, rows), BF16),
        pltpu.VMEM((side, side, CORES, tcols, rows), BF16),
        pltpu.VMEM((5, 8, LANES), F32), pltpu.VMEM((5, 8, LANES), F32),
        pltpu.VMEM((side, side, CORES, wr, k0), BF16), pltpu.VMEM((side, side, CORES, wr, k1), BF16), pltpu.VMEM((side, side, CORES, wr, k1), BF16),
        pltpu.VMEM((side, side, wr, k0), BF16), pltpu.VMEM((side, side, wr, k1), BF16), pltpu.VMEM((side, side, wr, k1), BF16),
        *reduce_bufs(k0), *reduce_bufs(k1), *reduce_bufs(k1),
        pltpu.SemaphoreType.DMA, pltpu.SemaphoreType.DMA((11,)),
        pltpu.SemaphoreType.DMA((2, chips)), pltpu.SemaphoreType.DMA((DX_PARTS, chips)),
        pltpu.SemaphoreType.DMA((3, 13)), pltpu.SemaphoreType.DMA((12,)), pltpu.SemaphoreType.DMA((5,)),
    ]
    wcat, tmine = pl.pallas_call(
        take,
        out_shape=(jax.ShapeDtypeStruct((wr, k0 + LANES + 2 * k1), BF16),
                   jax.ShapeDtypeStruct((CORES, side, side, tcols, rows), BF16)),
        in_specs=[hbm] * 7,
        out_specs=(vmem, vmem),
        scratch_shapes=[pltpu.VMEM((3, 1, wr), F32), pltpu.SemaphoreType.DMA((7,))],
        compiler_params=pltpu.CompilerParams(vmem_limit_bytes=TAKE_LIMIT),
        name="take",
    )(w_first, w_middle, w_last, u_first.reshape(1, wr), u_middle.reshape(1, wr), u_last.reshape(1, wr), target.T)
    outs = pl.pallas_call(
        functools.partial(kernel, n),
        out_shape=out_shape,
        in_specs=[hbm, vmem, vmem],
        out_specs=(vmem,) * len(out_shape),
        scratch_shapes=scratch,
        compiler_params=pltpu.CompilerParams(collective_id=0, has_side_effects=True, vmem_limit_bytes=VMEM_LIMIT),
        name="stack",
    )(acts_in, wcat, tmine)
    final = tuple(jax.ShapeDtypeStruct(shape, dtype) for shape, dtype in (
        ((1,), F32), ((total_rows, k0), BF16), ((wr, k0), F32), ((wr, k1), F32), ((wr, k1), F32),
        ((wr,), F32), ((wr,), F32), ((wr,), F32), ((k0,), BF16), ((k1,), BF16), ((k1,), BF16), ((3,), F32)))
    return pl.pallas_call(
        emit,
        out_shape=final,
        in_specs=[vmem] * len(final),
        out_specs=tuple(hbm if 1 <= i <= 4 else vmem for i in range(len(final))),
        scratch_shapes=[pltpu.SemaphoreType.DMA((4,))],
        compiler_params=pltpu.CompilerParams(vmem_limit_bytes=EMIT_LIMIT),
        name="emit",
    )(*outs)


def take(w0_hbm, w1_hbm, w2_hbm, u0_hbm, u1_hbm, u2_hbm, target_hbm, wcat, tmine, ubuf, sems):
    wr, k0 = w0_hbm.shape
    k1 = w1_hbm.shape[1]
    cores, side = tmine.shape[:2]
    rows = tmine.shape[-1]
    wide = k0 + LANES
    loads = [pltpu.make_async_copy(ref, ubuf.at[i], sems.at[i]) for i, ref in enumerate((u0_hbm, u1_hbm, u2_hbm))]
    for i, (ref, lo) in enumerate(((w0_hbm, 0), (w1_hbm, wide), (w2_hbm, wide + k1))):
        loads.append(pltpu.make_async_copy(ref, wcat.at[:, pl.ds(lo, ref.shape[1])], sems.at[3 + i]))
    for load in loads:
        load.start()

    def turn(j, carry):
        chip = j // cores
        part = tmine.at[lax.rem(j, cores), chip // side, lax.rem(chip, side)]
        pltpu.make_async_copy(target_hbm.at[:, pl.ds(pl.multiple_of(j * rows, rows), rows)], part, sems.at[6]).start()
        return carry

    lax.fori_loop(0, cores * side * side, turn, 0)
    lane = lax.broadcasted_iota(jnp.int32, (wr, LANES), 1)
    eye = (lax.broadcasted_iota(jnp.int32, (wr, wr), 0) == lax.broadcasted_iota(jnp.int32, (wr, wr), 1))
    uext = jnp.zeros((wr, LANES), F32)
    for i in range(3):
        loads[i].wait()
        column = jnp.sum(jnp.where(eye, jnp.broadcast_to(ubuf[i], (wr, wr)), 0.0), axis=1, keepdims=True)
        uext = jnp.where(lane == i, column, uext)
    wcat[:, pl.ds(k0, LANES)] = uext.astype(BF16)
    for load in loads[3:]:
        load.wait()
    pltpu.make_async_copy(tmine, tmine, sems.at[6]).wait()


def emit(*refs):
    count = (len(refs) - 1) // 2
    ins, outs, sems = refs[:count], refs[count:2 * count], refs[-1]
    copies = [pltpu.make_async_copy(ins[i], outs[i], sems.at[i - 1]) for i in range(1, 5)]
    for copy in copies:
        copy.start()
    for i in (0, *range(5, count)):
        outs[i][...] = ins[i][0, 0:outs[i].shape[0]]
    for copy in copies:
        copy.wait()


def solution(mesh):
    n = mesh.shape["model"]
    row_spec = P("rep", None)
    weight_spec = P(("rep", "model"), None)
    vector_spec = P(("rep", "model"))
    group_spec = P("rep")
    in_specs = (row_spec, weight_spec, weight_spec, weight_spec, vector_spec, vector_spec, vector_spec, P("rep", "model"))
    out_specs = (group_spec, row_spec, weight_spec, weight_spec, weight_spec, vector_spec, vector_spec, vector_spec, group_spec, group_spec, group_spec, group_spec)
    return jax.shard_map(lambda *args: device_program(n, *args), mesh=mesh, in_specs=in_specs, out_specs=out_specs, check_vma=False)
```

time: 735 us -> 98.6 us (0.13)
  waiting for transfers between devices: 373 us -> 0 us
  blocking collectives: 229 us -> 0 us
  Pallas kernels: 0 us -> 95.5 us
  matrix products: 91.5 us -> 0 us
  between operations: 24.1 us -> 0.83 us
    psum x5 -> x0, blocking collectives: 229 us -> none  [the longest x2 93.8 us: power_steps(): lax.psum(jnp.dot(u_vec.astype(jnp.bfloat16), w_local, preferred_element_t...]
    reduce_scatter x2 -> x0, waiting for transfers between devices: 212 us -> none  [device_program(): lax.psum_scatter(share_in, 'model', scatter_dimension=1, tiled=True)]
    all_gather x2 -> x0, waiting for transfers between devices: 131 us -> none  [device_program(): layer_in.append(lax.all_gather(act_local, 'model', axis=1, tiled=True))]
    pallas_call x0 -> x3, Pallas kernels: none -> 95.5 us  [the longest x1 88.5 us: device_program(): pl.pallas_call(functools.partial(kernel, n), out_shape=out_shape, in_spec...]
    dot_general x21 -> x0, matrix products: 91.5 us -> none  [the longest x3 30.5 us: device_program(): lax.dot_general(grad_low, layer_in[layer], BATCH_DIMS, preferred_element_...]
    psum x1 -> x0, waiting for transfers between devices: 29.3 us -> none  [device_program(): grad_in = lax.psum(share_in, 'model')]
  transfers between devices with their start and end apart: 5 -> 0, of which waited for: 5 -> 0; matrix products, arithmetic and copies ran while one was open for 5% -> 0% of each run, Pallas kernels for 0% -> 0%
where the time goes in v3:
time: 98.6 us; the launch traced here: 98.3 us
  Pallas kernels  95.5 us (97%)
  local copies, waits for them, and re-layouts  1.95 us (2%)
    pallas_call x1, Pallas kernels, device_program(): pl.pallas_call(functools.partial(kernel, n), out_shape=out_shape, in_spec...  88.5 us
    pallas_call x1, Pallas kernels, device_program(): pl.pallas_call(emit, out_shape=final, in_specs=[vmem] * len(final), out_s...  4.73 us
    pallas_call x1, Pallas kernels, device_program(): pl.pallas_call(take, out_shape=(jax.ShapeDtypeStruct((wr, k0 + LANES + 2...  2.3 us

profile of v3, /device:TPU:97, one launch (start us, length us, event | category | flops | bytes accessed | tf_op | source)
XLA Modules:
  0.0 98.3 jit_solution(253578051178994788)
XLA Ops:
  0.6 2.3 %take.1 = (bf16[32,2688]{1,0:T(8,128)(2,1)}, bf16[2,4,4,32,256]{4,3,2,1,0:T(8,128)(2,1)}) custom-call(bf16[32,512]{1,0:T(8,128)(2,1)} %w0_hbm.1, bf16[32,1024]{1,0:T(8,128)(2,1)} %w1_hbm.1, bf16[32,1024]{1,0:T(8,128)(2,1)} %w2_hbm.1, f32[1,32]{1,0:T(1,128)} %bitcast.5, f32[1,32]{1,0:T(1,128)} %bitcast.6, f32[1,32]{1,0:T(1,128)} %bitcast.7, ...), custom_call_target="tpu_custom_call" | custom-call | tf_op jit(solution)/shard_map/take/pallas_call | solution.py:649
  3.0 0.0 copy-start
  3.0 1.0 %copy-done = bf16[2,4,4,32,256]{4,3,2,1,0:T(8,128)(2,1)S(1)} copy-done((bf16[2,4,4,32,256]{4,3,2,1,0:T(8,128)(2,1)S(1)}, bf16[2,4,4,32,256]{4,3,2,1,0:T(8,128)(2,1)}, u32[]{:S(2)}) %copy-start) | copy-done | bytes 524312
  4.0 0.0 copy-start.1
  4.0 0.9 copy-done.1
  4.9 88.5 %stack.1 = (f32[1,1]{1,0:T(1,128)}, bf16[8192,512]{1,0:T(8,128)(2,1)S(1)}, f32[32,512]{1,0:T(8,128)S(1)}, f32[32,1024]{1,0:T(8,128)S(1)}, f32[32,1024]{1,0:T(8,1...) custom-call(bf16[8192,512]{1,0:T(8,128)(2,1)} %acts_hbm.1, ...), custom_call_target="tpu_custom_call" | custom-call | tf_op jit(solution)/shard_map/stack/pallas_call | solution.py:659
  93.4 4.7 %emit.1 = (f32[1]{0:T(128)}, bf16[8192,512]{1,0:T(8,128)(2,1)}, f32[32,512]{1,0:T(8,128)}, f32[32,1024]{1,0:T(8,128)}, f32[32,1024]{1,0:T(8,128)}, /*index=5*/f3...) custom-call(f32[1,1]{1,0:T(1,128)} %get-tuple-element.28.refs_0_, ...), custom_call_target="tpu_custom_call" | custom-call | tf_op jit(solution)/shard_map/emit/pallas_call | solution.py:671
Async XLA Ops:
  3.0 1.0 %copy-start = (bf16[2,4,4,32,256]{4,3,2,1,0:T(8,128)(2,1)S(1)}, bf16[2,4,4,32,256]{4,3,2,1,0:T(8,128)(2,1)}, u32[]{:S(2)}) copy-start(bf16[2,4,4,32,256]{4,3,2,1,0:T(8,128)(2,1)} %get-tuple-element.27.tmine) | copy-start | bytes 1572868
  4.0 0.9 copy-start.1

commit v4 on v3

--- a/solution.py
+++ b/solution.py
@@ -16,13 +16,14 @@
 BF16 = jnp.bfloat16
 NN = (((1,), (0,)), ((), ()))
 NT = (((1,), (1,)), ((), ()))
+TN = (((0,), (0,)), ((), ()))
 CORES = 2
 LANES = 128
 SUB = 16
 TILE = 256
-FTILE = 512
+FTILE = 256
 VMEM_LIMIT = 40 * 1024 * 1024
-TAKE_LIMIT = 66338816
+EMIT_PARTS = 16
 EMIT_LIMIT = 12 * 1024 * 1024
 DX_PARTS = 2
 XP, XM, YP, YM = (1, 0), (-1, 0), (0, 1), (0, -1)
@@ -356,34 +357,54 @@
     return hi, mid, lo
 
 
-def kernel(n, acts_hbm, wcat, tmine,
+def kernel(n, acts_hbm, w0_hbm, w1_hbm, w2_hbm, u0_hbm, u1_hbm, u2_hbm, target_hbm,
            loss_ref, dx_ref, g0_ref, g1_ref, g2_ref, un0_ref, un1_ref, un2_ref, v0_ref, v1_ref, v2_ref, sig_ref,
-           wa, wb, x0, x1, x2, xt0, xt1, xt2, yt0, yt1, yt2, mt, mask0, mask1, lowt, low, low2, dxa, dxb, uc, sq, vbuf,
-           tstage, trelay, tmid, tfinal, losssent, lossgot,
+           wa, w1, w2, x0, x1, x2, xt0, xt1, xt2, yt0, yt1, yt2, mt, mask0, mask1, lowt, low, low2, dxa, dxb, uc, cu, vbuf, ustart,
+           ubuf, tmine, tstage, trelay, tmid, tfinal, losssent, lossgot,
            d0, d1, d2, m0, m1, m2,
            ra0, rb0, rc0, re0, rf0, ra1, rb1, rc1, re1, rf1, ra2, rb2, rc2, re2, rf2,
-           acts_sem, send_sems, w_recv, dx_recv, rs_recv, t_recv, l_recv):
+           local_sems, send_sems, w_recv, dx_recv, rs_recv, t_recv, l_recv):
     p = Place(n)
     side = p.side
     rows = x0.shape[0]
-    wr = wcat.shape[0]
+    wr = w0_hbm.shape[0]
     total_rows, k0 = dx_ref.shape
-    k1 = wb.shape[1]
-    wide = k0 + LANES
+    k1 = w1.shape[1]
     width = wa.shape[0]
     mine = pl.ds(pl.multiple_of(p.me * wr, wr), wr)
     w0 = wa.at[:, pl.ds(0, k0)]
     ucols = wa.at[:, pl.ds(k0, LANES)]
-    w1 = wa.at[:, pl.ds(wide, k1)]
-    w2 = wb
-
-    acts_load = pltpu.make_async_copy(acts_hbm.at[pl.ds(pl.multiple_of(p.me * rows, rows), rows)], x0, acts_sem)
+
+    loads = [
+        pltpu.make_async_copy(u0_hbm, ubuf.at[0], local_sems.at[0]),
+        pltpu.make_async_copy(u1_hbm, ubuf.at[1], local_sems.at[1]),
+        pltpu.make_async_copy(u2_hbm, ubuf.at[2], local_sems.at[2]),
+        pltpu.make_async_copy(w0_hbm, w0.at[mine], local_sems.at[3]),
+        pltpu.make_async_copy(w1_hbm, w1.at[mine], local_sems.at[4]),
+        pltpu.make_async_copy(w2_hbm, w2.at[mine], local_sems.at[5]),
+    ]
+    for load in loads:
+        load.start()
+    acts_load = pltpu.make_async_copy(acts_hbm.at[pl.ds(pl.multiple_of(p.me * rows, rows), rows)], x0, local_sems.at[6])
     acts_load.start()
+    for j in range(n):
+        part = tmine.at[j % CORES, j // (CORES * side), (j // CORES) % side]
+        pltpu.make_async_copy(target_hbm.at[:, pl.ds(j * rows, rows)], part, local_sems.at[7]).start()
 
     barrier = pltpu.get_barrier_semaphore()
     peers = [p.dev(way) for way in (XP, XM, YP, YM)] + [p.dev((0, 0), True)]
     for peer in peers:
         pl.semaphore_signal(barrier, inc=1, device_id={"model": peer}, device_id_type=MESH)
+    lane = lax.broadcasted_iota(jnp.int32, (wr, LANES), 1)
+    eye = (lax.broadcasted_iota(jnp.int32, (wr, wr), 0) == lax.broadcasted_iota(jnp.int32, (wr, wr), 1))
+    uext = jnp.zeros((wr, LANES), F32)
+    for i in range(3):
+        loads[i].wait()
+        column = jnp.sum(jnp.where(eye, jnp.broadcast_to(ubuf[i], (wr, wr)), 0.0), axis=1, keepdims=True)
+        uext = jnp.where(lane == i, column, uext)
+    ucols[mine, :] = uext.astype(BF16)
+    for load in loads[3:]:
+        load.wait()
     pl.semaphore_wait(barrier, len(peers))
 
     def gather_weight(i, ref):
@@ -394,16 +415,13 @@
         cuts = [LANES * ((tiles * k) // 4) for k in range(5)]
         return Gather(Link(p, send_sems.at[i], w_recv.at[i]), ref_at, lambda k: ref.at[pl.ds(0, k * wr)], cuts)
 
-    ga, gb = gather_weight(0, wa), gather_weight(1, wb)
-    for g, ref, lo in ((ga, wa, 0), (gb, wb, wa.shape[1])):
-        own = wcat.at[:, pl.ds(lo, ref.shape[1])]
-        g.step0(own)
-        ref[mine] = own[...]
-
-    spread = Spread(Link(p, send_sems.at[2], t_recv), [send_sems.at[k] for k in (2, 3, 4)], tmine, tstage, trelay, tmid, tfinal)
+    ga, gb, gc = (gather_weight(i, ref) for i, ref in enumerate((wa, w1, w2)))
+    for g in (ga, gb, gc):
+        g.step0()
+    pltpu.make_async_copy(tmine, tmine, local_sems.at[7]).wait()
+    spread = Spread(Link(p, send_sems.at[3], t_recv), [send_sems.at[k] for k in (3, 4, 5)], tmine, tstage, trelay, tmid, tfinal)
     spread.pair_send()
     eye_big = (lax.broadcasted_iota(jnp.int32, (TILE, TILE), 0) == lax.broadcasted_iota(jnp.int32, (TILE, TILE), 1)).astype(BF16)
-    eye_small = eye_big[0:SUB, 0:SUB]
 
     def turn(src, dst):
         for j in range(max(src.shape) // TILE):
@@ -413,25 +431,27 @@
             else:
                 dst[at, :] = dot(eye_big, src[:, at], NT).astype(BF16)
 
-    def power(i, w_ref):
-        picked = (lax.broadcasted_iota(jnp.int32, (SUB, LANES), 1) == i).astype(BF16)
-        u_row = dot(picked, ucols[...], NT).astype(BF16)
-        for step in range(POWER_STEPS):
-            pv = dot(u_row, w_ref[...], NN)
-            norm = jnp.sqrt(jnp.sum(pv * pv, axis=1, keepdims=True))
-            v16 = (pv / jnp.maximum(norm, NORM_FLOOR)).astype(BF16)
-            sv = dot(w_ref[...], v16, NT)
-            sigma = jnp.sqrt(jnp.sum(sv * sv, axis=0, keepdims=True))
-            ucol = sv / sigma
-            if step + 1 < POWER_STEPS:
-                u_row = dot(eye_small, ucol.astype(BF16), NT).astype(BF16)
-        uc[i] = ucol
-        vbuf[i, :, pl.ds(0, v16.shape[1])] = v16
-        sigma = sigma[0:1, 0:1]
+    def start_rows():
+        picked = (lax.broadcasted_iota(jnp.int32, (SUB, LANES), 1) == lax.broadcasted_iota(jnp.int32, (SUB, LANES), 0)).astype(BF16)
+        ustart[...] = dot(picked, ucols[...], NT)
+
+    def power(i, w_ref, step):
+        u_row = (jnp.broadcast_to(ustart[i:i + 1, :], (SUB, width)) if step == 0 else uc[i]).astype(BF16)
+        pv = dot(u_row, w_ref[...], NN)
+        norm = jnp.sqrt(jnp.sum(pv * pv, axis=1, keepdims=True))
+        v16 = (pv / jnp.maximum(norm, NORM_FLOOR)).astype(BF16)
+        sv = dot(v16, w_ref[...], NT)
+        sigma = jnp.sqrt(jnp.sum(sv * sv, axis=1, keepdims=True))
+        uc[i] = sv / sigma
+        if step + 1 == POWER_STEPS:
+            vbuf[i, :, pl.ds(0, v16.shape[1])] = v16
+        return sigma[0:1, 0:1]
+
+    def finish_power(i, w_ref, sigma):
+        v16 = vbuf[i, :, pl.ds(0, w_ref.shape[1])]
         own = dot(v16, w_ref[mine, :], NT) / sigma
         (un0_ref, un1_ref, un2_ref)[i][...] = own[0:1]
         (v0_ref, v1_ref, v2_ref)[i][...] = v16[0:1]
-        return sigma
 
     def forward(w_ref, xt_ref, inv, y_ref, next_ref, mask_ref):
         for j in range(width // FTILE):
@@ -446,31 +466,38 @@
     turn(x0, xt0)
     ga.step1()
     gb.step1()
+    ga.step2()
+    gc.step1()
     spread.pair_take()
-    ga.step2()
+    ga.step3()
     gb.step2()
     spread.first_send()
-    ga.step3()
+    ga.step4()
+    gc.step2()
     gb.step3()
-    ga.step4()
     spread.first_relay()
     ga.finish()
-    sa = power(0, w0)
+    start_rows()
+    power(0, wa.at[:, pl.ds(0, k0)], 0)
+    gb.step4()
+    gc.step3()
+    spread.second_send()
+    sa = power(0, wa.at[:, pl.ds(0, k0)], 1)
     inva = 1.0 / sa
-    spread.second_send()
-    gb.step4()
     forward(w0, xt0, inva, yt0, xt1, mt)
-    turn(xt1, x1)
+    gc.step4()
+    gb.finish()
+    power(1, w1, 0)
+    spread.second_relay()
+    sb = power(1, w1, 1)
+    invb = 1.0 / sb
     turn(mt, mask0)
-    sb = power(1, w1)
-    spread.second_relay()
-    invb = 1.0 / sb
     forward(w1, xt1, invb, yt1, xt2, mt)
-    gb.finish()
-    sc = power(2, w2)
+    gc.finish()
+    power(2, w2, 0)
+    sc = power(2, w2, 1)
     invc = 1.0 / sc
     forward(w2, xt2, invc, yt2, None, None)
-    turn(xt2, x2)
     turn(mt, mask1)
     spread.finish()
 
@@ -493,25 +520,24 @@
         lowt[at, :] = g.astype(BF16)
         loss = loss + down(residual * residual)
         corr = corr + down(g * y)
-    whole = Total(Link(p, send_sems.at[10], l_recv), losssent, lossgot)
+    whole = Total(Link(p, send_sems.at[9], l_recv), losssent, lossgot)
     whole.first(jnp.sum(loss, axis=1, keepdims=True))
 
     def share(i, x_ref, d_ref, corr):
         corr = jnp.sum(corr, axis=1, keepdims=True)
-        parts = split3(uc[i] * (-corr))
-        lane = lax.broadcasted_iota(jnp.int32, (width, SUB), 1)
-        uu = jnp.zeros((width, SUB), F32)
-        for k, part in enumerate(parts):
-            uu = jnp.where(lane == k, part.astype(F32), uu)
-        sq[...] = uu.astype(BF16)
-
-        def body(j, carry):
-            at = pl.ds(pl.multiple_of(j * TILE, TILE), TILE)
-            full = dot(lowt[...], x_ref[:, at], NN) + dot(sq[...], vbuf[i, :, at], NN)
-            d_ref[:, :, :, :, at] = full.astype(BF16).reshape(side, side, CORES, wr, TILE)
-            return carry
-
-        lax.fori_loop(0, x_ref.shape[1] // TILE, body, 0)
+        sub = lax.broadcasted_iota(jnp.int32, (SUB, width), 0)
+        uu = jnp.zeros((SUB, width), F32)
+        for k, part in enumerate(split3(uc[i] * corr)):
+            uu = jnp.where(sub == k, part.astype(F32), uu)
+        ones = (lax.broadcasted_iota(jnp.int32, (SUB, LANES), 0) < 3).astype(BF16)
+        cu[...] = dot(uu.astype(BF16), ones, TN)
+        for j in range(x_ref.shape[1] // TILE):
+            full = dot(lowt[...], x_ref[:, pl.ds(j * TILE, TILE)], NN)
+            for k in range(TILE // LANES):
+                at = pl.ds(j * TILE + k * LANES, LANES)
+                v = vbuf[i, :, at].astype(F32)[0:1]
+                part = full[:, k * LANES:(k + 1) * LANES] - cu[...] * v
+                d_ref[:, :, :, :, at] = part.astype(BF16).reshape(side, side, CORES, wr, LANES)
 
     def back(w_ref, inv, low_ref, out_ref, mask_ref, next_ref):
         for j in range(w_ref.shape[1] // TILE):
@@ -532,7 +558,7 @@
         return corr
 
     def reducer(i, blocks, mate, relay, main, relay2, main2, acc, cols):
-        return Reduce(Link(p, send_sems.at[5 + i], rs_recv.at[i]), blocks, mate, relay, main, relay2, main2, acc, cols)
+        return Reduce(Link(p, send_sems.at[6 + i], rs_recv.at[i]), blocks, mate, relay, main, relay2, main2, acc, cols)
 
     rc = reducer(2, d2, m2, ra2, rb2, rc2, re2, rf2, k1)
     rb = reducer(1, d1, m1, ra1, rb1, rc1, re1, rf1, k1)
@@ -549,12 +575,14 @@
         def dx_at(dev, s, i=i):
             return dx_ref.at[pl.ds(pl.multiple_of(dev * rows + (i * part + s[0]), SUB), s[1] - s[0])]
 
-        gd.append(Gather(Link(p, send_sems.at[8 + i], dx_recv.at[i]), dx_at, lambda k: dx_ref.at[pl.ds(0, k * part)], [part * k // 4 for k in range(5)]))
+        gd.append(Gather(Link(p, send_sems.at[10 + i], dx_recv.at[i]), dx_at, lambda k: dx_ref.at[pl.ds(0, k * part)], [part * k // 4 for k in range(5)]))
     for g in gd:
         g.step0()
+    turn(xt2, x2)
     share(2, x2, d2, corr)
     rc.pair_send()
     corr = columns(dxa, yt1)
+    turn(xt1, x1)
     share(1, x1, d1, corr)
     rb.pair_send()
     rc.pair_add()
@@ -574,32 +602,35 @@
     rb.far_add()
     ra.far_add()
     whole.step(2)
+    gd[0].step2()
     rc.near_add()
     rb.near_add()
+    whole.step(3)
+    gd[1].step2()
     ra.near_add()
-    whole.step(3)
-    gd[0].step2()
+    gd[0].step3()
     rc.far2_add()
     rb.far2_add()
     ra.far2_add()
     loss_ref[...] = whole.step(4)[0:1, 0:1] * (0.5 * scale)
-    gd[1].step2()
+    gd[1].step3()
+    for i, (ref, sigma) in enumerate(((w0, sa), (w1, sb), (w2, sc))):
+        finish_power(i, ref, sigma)
+    gd[0].step4()
+    gd[1].step4()
     rc.finish(g2_ref, invc)
     rb.finish(g1_ref, invb)
     ra.finish(g0_ref, inva)
-    gd[0].step3()
-    gd[1].step3()
-    gd[0].step4()
-    gd[1].step4()
     for g in gd:
         g.finish()
     ga.drain()
     gb.drain()
+    gc.drain()
     spread.drain()
     whole.drain()
     ra.link.drain(dx_ref.at[pl.ds(0, (n - 1) * wr)])
-    rb.link.drain(wb.at[pl.ds(0, (n - 1) * wr)])
-    rc.link.drain(wb.at[pl.ds(0, (n - 1) * wr)])
+    rb.link.drain(w1.at[pl.ds(0, (n - 1) * wr)])
+    rc.link.drain(w1.at[pl.ds(0, (n - 1) * wr)])
     for g in gd:
         g.drain()
 
@@ -627,44 +658,37 @@
         jax.ShapeDtypeStruct((1, k0), BF16), jax.ShapeDtypeStruct((1, k1), BF16), jax.ShapeDtypeStruct((1, k1), BF16),
         jax.ShapeDtypeStruct((1, LANES), F32))
     scratch = [
-        pltpu.VMEM((width, k0 + LANES + k1), BF16), pltpu.VMEM((width, k1), BF16),
+        pltpu.VMEM((width, k0 + LANES), BF16), pltpu.VMEM((width, k1), BF16), pltpu.VMEM((width, k1), BF16),
         pltpu.VMEM((rows, k0), BF16), pltpu.VMEM((rows, k1), BF16), pltpu.VMEM((rows, k1), BF16),
         pltpu.VMEM((k0, rows), BF16), pltpu.VMEM((k1, rows), BF16), pltpu.VMEM((k1, rows), BF16),
         pltpu.VMEM((width, rows), F32), pltpu.VMEM((width, rows), F32), pltpu.VMEM((width, rows), F32),
         pltpu.VMEM((width, rows), BF16), pltpu.VMEM((rows, width), BF16), pltpu.VMEM((rows, width), BF16),
         pltpu.VMEM((width, rows), BF16), pltpu.VMEM((rows, width), BF16), pltpu.VMEM((rows, width), BF16),
         pltpu.VMEM((rows, width), BF16), pltpu.VMEM((rows, width), BF16),
-        pltpu.VMEM((3, width, SUB), F32), pltpu.VMEM((width, SUB), BF16), pltpu.VMEM((3, SUB, k1), BF16),
-        pltpu.VMEM((CORES, side, side, tcols, rows), BF16),
+        pltpu.VMEM((3, SUB, width), F32), pltpu.VMEM((width, LANES), F32), pltpu.VMEM((3, SUB, k1), BF16), pltpu.VMEM((SUB, width), F32),
+        pltpu.VMEM((3, 1, wr), F32),
+        pltpu.VMEM((CORES, side, side, tcols, rows), BF16), pltpu.VMEM((CORES, side, side, tcols, rows), BF16),
         pltpu.VMEM((4, 2, side // 2, tcols, rows), BF16), pltpu.VMEM((2, side, side, tcols, rows), BF16),
         pltpu.VMEM((side, side, CORES, tcols, rows), BF16),
         pltpu.VMEM((5, 8, LANES), F32), pltpu.VMEM((5, 8, LANES), F32),
         pltpu.VMEM((side, side, CORES, wr, k0), BF16), pltpu.VMEM((side, side, CORES, wr, k1), BF16), pltpu.VMEM((side, side, CORES, wr, k1), BF16),
         pltpu.VMEM((side, side, wr, k0), BF16), pltpu.VMEM((side, side, wr, k1), BF16), pltpu.VMEM((side, side, wr, k1), BF16),
         *reduce_bufs(k0), *reduce_bufs(k1), *reduce_bufs(k1),
-        pltpu.SemaphoreType.DMA, pltpu.SemaphoreType.DMA((11,)),
-        pltpu.SemaphoreType.DMA((2, chips)), pltpu.SemaphoreType.DMA((DX_PARTS, chips)),
+        pltpu.SemaphoreType.DMA((8,)), pltpu.SemaphoreType.DMA((10 + DX_PARTS,)),
+        pltpu.SemaphoreType.DMA((3, chips)), pltpu.SemaphoreType.DMA((DX_PARTS, chips)),
         pltpu.SemaphoreType.DMA((3, 13)), pltpu.SemaphoreType.DMA((12,)), pltpu.SemaphoreType.DMA((5,)),
     ]
-    wcat, tmine = pl.pallas_call(
-        take,
-        out_shape=(jax.ShapeDtypeStruct((wr, k0 + LANES + 2 * k1), BF16),
-                   jax.ShapeDtypeStruct((CORES, side, side, tcols, rows), BF16)),
-        in_specs=[hbm] * 7,
-        out_specs=(vmem, vmem),
-        scratch_shapes=[pltpu.VMEM((3, 1, wr), F32), pltpu.SemaphoreType.DMA((7,))],
-        compiler_params=pltpu.CompilerParams(vmem_limit_bytes=TAKE_LIMIT),
-        name="take",
-    )(w_first, w_middle, w_last, u_first.reshape(1, wr), u_middle.reshape(1, wr), u_last.reshape(1, wr), target.T)
+    small = (w_first, w_middle, w_last, u_first.reshape(1, wr), u_middle.reshape(1, wr), u_last.reshape(1, wr), target.T)
+    small = [pltpu.with_memory_space_constraint(a, pltpu.HBM) for a in small]
     outs = pl.pallas_call(
         functools.partial(kernel, n),
         out_shape=out_shape,
-        in_specs=[hbm, vmem, vmem],
+        in_specs=[hbm] * 8,
         out_specs=(vmem,) * len(out_shape),
         scratch_shapes=scratch,
         compiler_params=pltpu.CompilerParams(collective_id=0, has_side_effects=True, vmem_limit_bytes=VMEM_LIMIT),
         name="stack",
-    )(acts_in, wcat, tmine)
+    )(acts_in, *small)
     final = tuple(jax.ShapeDtypeStruct(shape, dtype) for shape, dtype in (
         ((1,), F32), ((total_rows, k0), BF16), ((wr, k0), F32), ((wr, k1), F32), ((wr, k1), F32),
         ((wr,), F32), ((wr,), F32), ((wr,), F32), ((k0,), BF16), ((k1,), BF16), ((k1,), BF16), ((3,), F32)))
@@ -673,48 +697,18 @@
         out_shape=final,
         in_specs=[vmem] * len(final),
         out_specs=tuple(hbm if 1 <= i <= 4 else vmem for i in range(len(final))),
-        scratch_shapes=[pltpu.SemaphoreType.DMA((4,))],
+        scratch_shapes=[pltpu.SemaphoreType.DMA((3 + EMIT_PARTS,))],
         compiler_params=pltpu.CompilerParams(vmem_limit_bytes=EMIT_LIMIT),
         name="emit",
     )(*outs)
 
 
-def take(w0_hbm, w1_hbm, w2_hbm, u0_hbm, u1_hbm, u2_hbm, target_hbm, wcat, tmine, ubuf, sems):
-    wr, k0 = w0_hbm.shape
-    k1 = w1_hbm.shape[1]
-    cores, side = tmine.shape[:2]
-    rows = tmine.shape[-1]
-    wide = k0 + LANES
-    loads = [pltpu.make_async_copy(ref, ubuf.at[i], sems.at[i]) for i, ref in enumerate((u0_hbm, u1_hbm, u2_hbm))]
-    for i, (ref, lo) in enumerate(((w0_hbm, 0), (w1_hbm, wide), (w2_hbm, wide + k1))):
-        loads.append(pltpu.make_async_copy(ref, wcat.at[:, pl.ds(lo, ref.shape[1])], sems.at[3 + i]))
-    for load in loads:
-        load.start()
-
-    def turn(j, carry):
-        chip = j // cores
-        part = tmine.at[lax.rem(j, cores), chip // side, lax.rem(chip, side)]
-        pltpu.make_async_copy(target_hbm.at[:, pl.ds(pl.multiple_of(j * rows, rows), rows)], part, sems.at[6]).start()
-        return carry
-
-    lax.fori_loop(0, cores * side * side, turn, 0)
-    lane = lax.broadcasted_iota(jnp.int32, (wr, LANES), 1)
-    eye = (lax.broadcasted_iota(jnp.int32, (wr, wr), 0) == lax.broadcasted_iota(jnp.int32, (wr, wr), 1))
-    uext = jnp.zeros((wr, LANES), F32)
-    for i in range(3):
-        loads[i].wait()
-        column = jnp.sum(jnp.where(eye, jnp.broadcast_to(ubuf[i], (wr, wr)), 0.0), axis=1, keepdims=True)
-        uext = jnp.where(lane == i, column, uext)
-    wcat[:, pl.ds(k0, LANES)] = uext.astype(BF16)
-    for load in loads[3:]:
-        load.wait()
-    pltpu.make_async_copy(tmine, tmine, sems.at[6]).wait()
-
-
 def emit(*refs):
     count = (len(refs) - 1) // 2
     ins, outs, sems = refs[:count], refs[count:2 * count], refs[-1]
-    copies = [pltpu.make_async_copy(ins[i], outs[i], sems.at[i - 1]) for i in range(1, 5)]
+    part = ins[1].shape[0] // EMIT_PARTS
+    copies = [pltpu.make_async_copy(ins[1].at[pl.ds(k * part, part)], outs[1].at[pl.ds(k * part, part)], sems.at[3 + k]) for k in range(EMIT_PARTS)]
+    copies += [pltpu.make_async_copy(ins[i], outs[i], sems.at[i - 2]) for i in range(2, 5)]
     for copy in copies:
         copy.start()
     for i in (0, *range(5, count)):

time: 98.6 us -> 83 us (0.84)
  Pallas kernels: 95.5 us -> 82.1 us
  local copies, waits for them, and re-layouts: 1.95 us -> 0 us
    pallas_call x1, Pallas kernels: 88.5 us -> 77.4 us  [device_program(): pl.pallas_call(functools.partial(kernel, n), out_shape=out_shape, in_spec...]
    pallas_call x1 -> x0, Pallas kernels: 2.3 us -> none  [device_program(): pl.pallas_call(take, out_shape=(jax.ShapeDtypeStruct((wr, k0 + LANES + 2...]
    unnamed x4 -> x0, local copies, waits for them, and re-layouts: 1.95 us -> none
where the time goes in v4:
time: 83 us; the launch traced here: 82.9 us
  Pallas kernels  82.1 us (99%)
    pallas_call x1, Pallas kernels, device_program(): pl.pallas_call(functools.partial(kernel, n), out_shape=out_shape, in_spec...  77.4 us
    pallas_call x1, Pallas kernels, device_program(): pl.pallas_call(emit, out_shape=final, in_specs=[vmem] * len(final), out_s...  4.69 us

profile of v4, /device:TPU:97, one launch (start us, length us, event | category | flops | bytes accessed | tf_op | source)
XLA Modules:
  0.0 82.9 jit_solution(14780699230944938252)
XLA Ops:
  0.6 77.4 %stack.1 = (f32[1,1]{1,0:T(1,128)}, bf16[8192,512]{1,0:T(8,128)(2,1)S(1)}, f32[32,512]{1,0:T(8,128)S(1)}, f32[32,1024]{1,0:T(8,128)S(1)}, f32[32,1024]{1,0:T(8,1...) custom-call(bf16[8192,512]{1,0:T(8,128)(2,1)} %acts_hbm.1, ...), custom_call_target="tpu_custom_call" | custom-call | tf_op jit(solution)/shard_map/stack/pallas_call | solution.py:683
  78.1 4.7 %emit.1 = (f32[1]{0:T(128)}, bf16[8192,512]{1,0:T(8,128)(2,1)}, f32[32,512]{1,0:T(8,128)}, f32[32,1024]{1,0:T(8,128)}, f32[32,1024]{1,0:T(8,128)}, /*index=5*/f3...) custom-call(f32[1,1]{1,0:T(1,128)} %get-tuple-element.24.refs_0_, ...), custom_call_target="tpu_custom_call" | custom-call | tf_op jit(solution)/shard_map/emit/pallas_call | solution.py:695

commit v5 on v4

--- a/solution.py
+++ b/solution.py
@@ -23,10 +23,12 @@
 TILE = 256
 FTILE = 256
 VMEM_LIMIT = 40 * 1024 * 1024
-EMIT_PARTS = 16
 EMIT_LIMIT = 12 * 1024 * 1024
 DX_PARTS = 2
 XP, XM, YP, YM = (1, 0), (-1, 0), (0, 1), (0, -1)
+HERE = (0, 0)
+FAR = 2
+TRAIL = 1
 
 
 def dot(lhs, rhs, dims):
@@ -48,9 +50,11 @@
     def row(self, dy):
         return lax.rem(self.y + (dy + self.side), self.side)
 
-    def dev(self, rel, other=False):
-        core = 1 - self.core if other else self.core
-        return (self.row(rel[1]) * self.side + self.col(rel[0])) * CORES + core
+    def dev(self, rel):
+        return self.at(self.col(rel[0]), self.row(rel[1]))
+
+    def mate(self):
+        return self.me + 1 - CORES * self.core
 
     def at(self, x, y):
         return (y * self.side + x) * CORES + self.core
@@ -74,10 +78,10 @@
         self.copy(i, src, dst, target, send_sem).start()
 
     def wait(self, i, dst):
-        self.copy(i, dst, dst, self.place.dev((0, 0), True)).wait_recv()
+        self.copy(i, dst, dst, self.place.mate()).wait_recv()
 
     def drain(self, sent, send_sem=None):
-        self.copy(0, sent, sent, self.place.dev((0, 0), True), send_sem).wait_send()
+        self.copy(0, sent, sent, self.place.mate(), send_sem).wait_send()
 
 
 class Gather:
@@ -92,18 +96,18 @@
     def number(self, rel):
         return (rel[1] + 1) * self.place.side + rel[0] + 1
 
-    def start(self, rel, spans, way, src=None):
+    def start(self, rel, spans, way):
         there = self.number(self.place.norm((rel[0] - way[0], rel[1] - way[1])))
         for s in spans:
             ref = self.ref_at(self.place.dev(rel), s)
-            self.link.start(there, ref if src is None else src, ref, self.place.dev(way))
+            self.link.start(there, ref, ref, self.place.dev(way))
 
     def take(self, rel):
         self.link.wait(self.number(rel), self.ref_at(self.place.dev(rel), self.full[0]))
 
-    def mate(self, rel, src=None):
+    def mate(self, rel):
         ref = self.ref_at(self.place.dev(rel), self.full[0])
-        self.link.start(self.number((0, 0)), ref if src is None else src, ref, self.place.dev((0, 0), True))
+        self.link.start(self.number(HERE), ref, ref, self.place.mate())
 
     def cross(self, rel, axis):
         for way in ((YP, YM) if axis == "x" else (XP, XM)):
@@ -114,10 +118,10 @@
         way = {("x", -1): XP, ("x", 1): XM, ("y", -1): YP, ("y", 1): YM}[(axis, off)]
         self.start(rel, (self.fwd if off < 0 else self.bwd)[first], way)
 
-    def step0(self, src=None):
+    def step0(self):
         for way in (XP, YP, XM, YM):
-            self.start((0, 0), self.full, way, src)
-        self.mate((0, 0), src)
+            self.start(HERE, self.full, way)
+        self.mate(HERE)
 
     def step1(self):
         for way in (XP, YP, XM, YM):
@@ -152,7 +156,7 @@
         self.mate((2, 2))
 
     def finish(self):
-        self.link.wait(self.number((0, 0)), self.bulk(self.place.side ** 2))
+        self.link.wait(self.number(HERE), self.bulk(self.place.side ** 2))
 
     def drain(self):
         self.link.drain(self.bulk(CORES * self.place.side ** 2 - 1))
@@ -178,7 +182,7 @@
 
     def pair_send(self):
         p = self.place
-        self.link.start(0, self.blocks.at[:, :, 1 - p.core], self.mate, p.dev((0, 0), True))
+        self.link.start(0, self.blocks.at[:, :, 1 - p.core], self.mate, p.mate())
 
     def pair_add(self):
         p = self.place
@@ -248,7 +252,7 @@
 
     def pair_send(self):
         p = self.place
-        self.link.start(0, self.mine.at[1 - p.core], self.stage.at[p.core], p.dev((0, 0), True), self.sems[0])
+        self.link.start(0, self.mine.at[1 - p.core], self.stage.at[p.core], p.mate(), self.sems[0])
 
     def pair_take(self):
         p = self.place
@@ -328,7 +332,7 @@
         self.link, self.place, self.sent, self.got = link, link.place, sent, got
         p = self.place
         odd = lambda c: c + 1 - 2 * lax.rem(c, 2)
-        self.targets = [p.dev((0, 0), True), p.at(odd(p.x), p.y), p.at(p.side - 1 - p.x, p.y), p.at(p.x, odd(p.y)), p.at(p.x, p.side - 1 - p.y)]
+        self.targets = [p.mate(), p.at(odd(p.x), p.y), p.at(p.side - 1 - p.x, p.y), p.at(p.x, odd(p.y)), p.at(p.x, p.side - 1 - p.y)]
 
     def send(self, i):
         self.link.start(i, self.sent.at[i], self.got.at[i], self.targets[i])
@@ -349,6 +353,14 @@
         self.link.drain(self.sent)
 
 
+def down(value):
+    return jnp.sum(value, axis=0, keepdims=True)
+
+
+def along(value):
+    return jnp.sum(value, axis=1, keepdims=True)
+
+
 def split3(value):
     hi = value.astype(BF16)
     rest = value - hi.astype(F32)
@@ -359,17 +371,18 @@
 
 def kernel(n, acts_hbm, w0_hbm, w1_hbm, w2_hbm, u0_hbm, u1_hbm, u2_hbm, target_hbm,
            loss_ref, dx_ref, g0_ref, g1_ref, g2_ref, un0_ref, un1_ref, un2_ref, v0_ref, v1_ref, v2_ref, sig_ref,
-           wa, w1, w2, x0, x1, x2, xt0, xt1, xt2, yt0, yt1, yt2, mt, mask0, mask1, lowt, low, low2, dxa, dxb, uc, cu, vbuf, ustart,
+           wa, wb, x0, x1, x2, xt0, xt1, xt2, yt0, yt1, yt2, mt, mask0, mask1, lowt, low, low2, dxa, dxb, uv, cu, ustart,
            ubuf, tmine, tstage, trelay, tmid, tfinal, losssent, lossgot,
            d0, d1, d2, m0, m1, m2,
            ra0, rb0, rc0, re0, rf0, ra1, rb1, rc1, re1, rf1, ra2, rb2, rc2, re2, rf2,
-           local_sems, send_sems, w_recv, dx_recv, rs_recv, t_recv, l_recv):
+           local_sems, send_sems, w_recv, dx_recv, rs_recv, t_recv, l_recv, o_recv):
     p = Place(n)
     side = p.side
     rows = x0.shape[0]
     wr = w0_hbm.shape[0]
     total_rows, k0 = dx_ref.shape
-    k1 = w1.shape[1]
+    k1 = wb.shape[2]
+    w1, w2 = wb.at[0], wb.at[1]
     width = wa.shape[0]
     mine = pl.ds(pl.multiple_of(p.me * wr, wr), wr)
     w0 = wa.at[:, pl.ds(0, k0)]
@@ -392,7 +405,7 @@
         pltpu.make_async_copy(target_hbm.at[:, pl.ds(j * rows, rows)], part, local_sems.at[7]).start()
 
     barrier = pltpu.get_barrier_semaphore()
-    peers = [p.dev(way) for way in (XP, XM, YP, YM)] + [p.dev((0, 0), True)]
+    peers = [p.dev(way) for way in (XP, XM, YP, YM)] + [p.mate()]
     for peer in peers:
         pl.semaphore_signal(barrier, inc=1, device_id={"model": peer}, device_id_type=MESH)
     lane = lax.broadcasted_iota(jnp.int32, (wr, LANES), 1)
@@ -400,7 +413,7 @@
     uext = jnp.zeros((wr, LANES), F32)
     for i in range(3):
         loads[i].wait()
-        column = jnp.sum(jnp.where(eye, jnp.broadcast_to(ubuf[i], (wr, wr)), 0.0), axis=1, keepdims=True)
+        column = along(jnp.where(eye, jnp.broadcast_to(ubuf[i], (wr, wr)), 0.0))
         uext = jnp.where(lane == i, column, uext)
     ucols[mine, :] = uext.astype(BF16)
     for load in loads[3:]:
@@ -435,20 +448,27 @@
         picked = (lax.broadcasted_iota(jnp.int32, (SUB, LANES), 1) == lax.broadcasted_iota(jnp.int32, (SUB, LANES), 0)).astype(BF16)
         ustart[...] = dot(picked, ucols[...], NT)
 
-    def power(i, w_ref, step):
-        u_row = (jnp.broadcast_to(ustart[i:i + 1, :], (SUB, width)) if step == 0 else uc[i]).astype(BF16)
-        pv = dot(u_row, w_ref[...], NN)
-        norm = jnp.sqrt(jnp.sum(pv * pv, axis=1, keepdims=True))
-        v16 = (pv / jnp.maximum(norm, NORM_FLOOR)).astype(BF16)
-        sv = dot(v16, w_ref[...], NT)
-        sigma = jnp.sqrt(jnp.sum(sv * sv, axis=1, keepdims=True))
-        uc[i] = sv / sigma
-        if step + 1 == POWER_STEPS:
-            vbuf[i, :, pl.ds(0, v16.shape[1])] = v16
-        return sigma[0:1, 0:1]
+    us, vs, ss = (pl.ds(k * SUB, SUB) for k in range(3))
+
+    def power(i, w_ref, start):
+        u_row = jnp.broadcast_to(start, (SUB, width)).astype(BF16)
+        for step in range(POWER_STEPS):
+            pv = dot(u_row, w_ref[...], NN)
+            norm = jnp.sqrt(along(pv * pv))
+            v16 = (pv / jnp.maximum(norm, NORM_FLOOR)).astype(BF16)
+            sv = dot(v16, w_ref[...], NT)
+            sigma = jnp.sqrt(along(sv * sv))
+            u16 = sv / sigma
+            u_row = u16.astype(BF16)
+        uv[i, us, :] = u16
+        uv[i, vs, pl.ds(0, v16.shape[1])] = v16.astype(F32)
+        uv[i, ss, pl.ds(0, LANES)] = jnp.broadcast_to(sigma, (SUB, LANES))
+
+    def sigma_of(i):
+        return uv[i, ss, pl.ds(0, LANES)][0:1, 0:1]
 
     def finish_power(i, w_ref, sigma):
-        v16 = vbuf[i, :, pl.ds(0, w_ref.shape[1])]
+        v16 = uv[i, vs, pl.ds(0, w_ref.shape[1])].astype(BF16)
         own = dot(v16, w_ref[mine, :], NT) / sigma
         (un0_ref, un1_ref, un2_ref)[i][...] = own[0:1]
         (v0_ref, v1_ref, v2_ref)[i][...] = v16[0:1]
@@ -468,34 +488,35 @@
     gb.step1()
     ga.step2()
     gc.step1()
+    gb.step2()
     spread.pair_take()
     ga.step3()
-    gb.step2()
     spread.first_send()
-    ga.step4()
     gc.step2()
     gb.step3()
+    ga.step4()
+    gc.step3()
+    gb.step4()
     spread.first_relay()
     ga.finish()
     start_rows()
-    power(0, wa.at[:, pl.ds(0, k0)], 0)
-    gb.step4()
-    gc.step3()
-    spread.second_send()
-    sa = power(0, wa.at[:, pl.ds(0, k0)], 1)
+    power(0, w0, ustart[0:1, :])
+    gc.step4()
+    sa = sigma_of(0)
     inva = 1.0 / sa
     forward(w0, xt0, inva, yt0, xt1, mt)
-    gc.step4()
+    turn(mt, mask0)
+    spread.second_send()
     gb.finish()
-    power(1, w1, 0)
+    gc.finish()
+    power(1 + p.core, wb.at[p.core], jnp.where(p.core == 0, ustart[1:2, :], ustart[2:3, :]))
+    other = Link(p, send_sems.at[10 + DX_PARTS], o_recv)
+    other.start(0, uv.at[1 + p.core], uv.at[1 + p.core], p.mate())
     spread.second_relay()
-    sb = power(1, w1, 1)
+    other.wait(0, uv.at[2 - p.core])
+    sb, sc = sigma_of(1), sigma_of(2)
     invb = 1.0 / sb
-    turn(mt, mask0)
     forward(w1, xt1, invb, yt1, xt2, mt)
-    gc.finish()
-    power(2, w2, 0)
-    sc = power(2, w2, 1)
     invc = 1.0 / sc
     forward(w2, xt2, invc, yt2, None, None)
     turn(mt, mask1)
@@ -507,8 +528,6 @@
     scale = 1.0 / total_rows
     zero_row = jnp.zeros((1, rows), F32)
 
-    def down(value):
-        return jnp.sum(value, axis=0, keepdims=True)
 
     loss = zero_row
     corr = zero_row
@@ -521,13 +540,13 @@
         loss = loss + down(residual * residual)
         corr = corr + down(g * y)
     whole = Total(Link(p, send_sems.at[9], l_recv), losssent, lossgot)
-    whole.first(jnp.sum(loss, axis=1, keepdims=True))
+    whole.first(along(loss))
 
     def share(i, x_ref, d_ref, corr):
-        corr = jnp.sum(corr, axis=1, keepdims=True)
+        corr = along(corr)
         sub = lax.broadcasted_iota(jnp.int32, (SUB, width), 0)
         uu = jnp.zeros((SUB, width), F32)
-        for k, part in enumerate(split3(uc[i] * corr)):
+        for k, part in enumerate(split3(uv[i, us, :] * corr)):
             uu = jnp.where(sub == k, part.astype(F32), uu)
         ones = (lax.broadcasted_iota(jnp.int32, (SUB, LANES), 0) < 3).astype(BF16)
         cu[...] = dot(uu.astype(BF16), ones, TN)
@@ -535,7 +554,7 @@
             full = dot(lowt[...], x_ref[:, pl.ds(j * TILE, TILE)], NN)
             for k in range(TILE // LANES):
                 at = pl.ds(j * TILE + k * LANES, LANES)
-                v = vbuf[i, :, at].astype(F32)[0:1]
+                v = uv[i, vs, at][0:1]
                 part = full[:, k * LANES:(k + 1) * LANES] - cu[...] * v
                 d_ref[:, :, :, :, at] = part.astype(BF16).reshape(side, side, CORES, wr, LANES)
 
@@ -597,27 +616,27 @@
     ra.pair_add()
     ra.far_send()
     whole.step(1)
+    gd[1].step1()
     rc.far_add()
-    gd[1].step1()
+    gd[0].step2()
     rb.far_add()
     ra.far_add()
     whole.step(2)
-    gd[0].step2()
     rc.near_add()
+    gd[1].step2()
     rb.near_add()
+    ra.near_add()
     whole.step(3)
-    gd[1].step2()
-    ra.near_add()
     gd[0].step3()
     rc.far2_add()
+    gd[1].step3()
     rb.far2_add()
     ra.far2_add()
+    gd[0].step4()
+    gd[1].step4()
     loss_ref[...] = whole.step(4)[0:1, 0:1] * (0.5 * scale)
-    gd[1].step3()
     for i, (ref, sigma) in enumerate(((w0, sa), (w1, sb), (w2, sc))):
         finish_power(i, ref, sigma)
-    gd[0].step4()
-    gd[1].step4()
     rc.finish(g2_ref, invc)
     rb.finish(g1_ref, invb)
     ra.finish(g0_ref, inva)
@@ -628,6 +647,7 @@
     gc.drain()
     spread.drain()
     whole.drain()
+    other.drain(uv.at[0])
     ra.link.drain(dx_ref.at[pl.ds(0, (n - 1) * wr)])
     rb.link.drain(w1.at[pl.ds(0, (n - 1) * wr)])
     rc.link.drain(w1.at[pl.ds(0, (n - 1) * wr)])
@@ -658,14 +678,14 @@
         jax.ShapeDtypeStruct((1, k0), BF16), jax.ShapeDtypeStruct((1, k1), BF16), jax.ShapeDtypeStruct((1, k1), BF16),
         jax.ShapeDtypeStruct((1, LANES), F32))
     scratch = [
-        pltpu.VMEM((width, k0 + LANES), BF16), pltpu.VMEM((width, k1), BF16), pltpu.VMEM((width, k1), BF16),
+        pltpu.VMEM((width, k0 + LANES), BF16), pltpu.VMEM((2, width, k1), BF16),
         pltpu.VMEM((rows, k0), BF16), pltpu.VMEM((rows, k1), BF16), pltpu.VMEM((rows, k1), BF16),
         pltpu.VMEM((k0, rows), BF16), pltpu.VMEM((k1, rows), BF16), pltpu.VMEM((k1, rows), BF16),
         pltpu.VMEM((width, rows), F32), pltpu.VMEM((width, rows), F32), pltpu.VMEM((width, rows), F32),
         pltpu.VMEM((width, rows), BF16), pltpu.VMEM((rows, width), BF16), pltpu.VMEM((rows, width), BF16),
         pltpu.VMEM((width, rows), BF16), pltpu.VMEM((rows, width), BF16), pltpu.VMEM((rows, width), BF16),
         pltpu.VMEM((rows, width), BF16), pltpu.VMEM((rows, width), BF16),
-        pltpu.VMEM((3, SUB, width), F32), pltpu.VMEM((width, LANES), F32), pltpu.VMEM((3, SUB, k1), BF16), pltpu.VMEM((SUB, width), F32),
+        pltpu.VMEM((3, 3 * SUB, width), F32), pltpu.VMEM((width, LANES), F32), pltpu.VMEM((SUB, width), F32),
         pltpu.VMEM((3, 1, wr), F32),
         pltpu.VMEM((CORES, side, side, tcols, rows), BF16), pltpu.VMEM((CORES, side, side, tcols, rows), BF16),
         pltpu.VMEM((4, 2, side // 2, tcols, rows), BF16), pltpu.VMEM((2, side, side, tcols, rows), BF16),
@@ -674,9 +694,9 @@
         pltpu.VMEM((side, side, CORES, wr, k0), BF16), pltpu.VMEM((side, side, CORES, wr, k1), BF16), pltpu.VMEM((side, side, CORES, wr, k1), BF16),
         pltpu.VMEM((side, side, wr, k0), BF16), pltpu.VMEM((side, side, wr, k1), BF16), pltpu.VMEM((side, side, wr, k1), BF16),
         *reduce_bufs(k0), *reduce_bufs(k1), *reduce_bufs(k1),
-        pltpu.SemaphoreType.DMA((8,)), pltpu.SemaphoreType.DMA((10 + DX_PARTS,)),
+        pltpu.SemaphoreType.DMA((8,)), pltpu.SemaphoreType.DMA((11 + DX_PARTS,)),
         pltpu.SemaphoreType.DMA((3, chips)), pltpu.SemaphoreType.DMA((DX_PARTS, chips)),
-        pltpu.SemaphoreType.DMA((3, 13)), pltpu.SemaphoreType.DMA((12,)), pltpu.SemaphoreType.DMA((5,)),
+        pltpu.SemaphoreType.DMA((3, 13)), pltpu.SemaphoreType.DMA((12,)), pltpu.SemaphoreType.DMA((5,)), pltpu.SemaphoreType.DMA((1,)),
     ]
     small = (w_first, w_middle, w_last, u_first.reshape(1, wr), u_middle.reshape(1, wr), u_last.reshape(1, wr), target.T)
     small = [pltpu.with_memory_space_constraint(a, pltpu.HBM) for a in small]
@@ -693,26 +713,26 @@
         ((1,), F32), ((total_rows, k0), BF16), ((wr, k0), F32), ((wr, k1), F32), ((wr, k1), F32),
         ((wr,), F32), ((wr,), F32), ((wr,), F32), ((k0,), BF16), ((k1,), BF16), ((k1,), BF16), ((3,), F32)))
     return pl.pallas_call(
-        emit,
+        functools.partial(emit, len(final)),
         out_shape=final,
         in_specs=[vmem] * len(final),
-        out_specs=tuple(hbm if 1 <= i <= 4 else vmem for i in range(len(final))),
-        scratch_shapes=[pltpu.SemaphoreType.DMA((3 + EMIT_PARTS,))],
+        out_specs=(hbm,) * len(final),
+        scratch_shapes=[pltpu.VMEM(f.shape, f.dtype) for f in final if len(f.shape) == 1] + [pltpu.SemaphoreType.DMA((len(final),))],
         compiler_params=pltpu.CompilerParams(vmem_limit_bytes=EMIT_LIMIT),
         name="emit",
     )(*outs)
 
 
-def emit(*refs):
-    count = (len(refs) - 1) // 2
-    ins, outs, sems = refs[:count], refs[count:2 * count], refs[-1]
-    part = ins[1].shape[0] // EMIT_PARTS
-    copies = [pltpu.make_async_copy(ins[1].at[pl.ds(k * part, part)], outs[1].at[pl.ds(k * part, part)], sems.at[3 + k]) for k in range(EMIT_PARTS)]
-    copies += [pltpu.make_async_copy(ins[i], outs[i], sems.at[i - 2]) for i in range(2, 5)]
+def emit(count, *refs):
+    ins, outs, small, sems = refs[:count], refs[count:CORES * count], refs[CORES * count:-1], refs[-1]
+    flat = [i for i in range(count) if len(outs[i].shape) < len(ins[i].shape)]
+    copies = [pltpu.make_async_copy(ins[i], outs[i], sems.at[i]) for i in range(count) if i not in flat]
     for copy in copies:
         copy.start()
-    for i in (0, *range(5, count)):
-        outs[i][...] = ins[i][0, 0:outs[i].shape[0]]
+    for i, buf in zip(flat, small):
+        buf[...] = ins[i][0, 0:outs[i].shape[0]]
+        copies.append(pltpu.make_async_copy(buf, outs[i], sems.at[i]))
+        copies[-1].start()
     for copy in copies:
         copy.wait()
 

time: 83 us -> 81.9 us (0.987)
  Pallas kernels: 82.1 us -> 81 us
where the time goes in v5:
time: 81.9 us; the launch traced here: 81.8 us
  Pallas kernels  81 us (99%)
  between operations  0.82 us (1%)
    pallas_call x1, Pallas kernels, device_program(): pl.pallas_call(functools.partial(kernel, n), out_shape=out_shape, in_spec...  76.8 us
    pallas_call x1, Pallas kernels, device_program(): pl.pallas_call(functools.partial(emit, len(final)), out_shape=final, in_s...  4.16 us

profile of v5, /device:TPU:97, one launch (start us, length us, event | category | flops | bytes accessed | tf_op | source)
XLA Modules:
  0.0 81.8 jit_solution(7167872659617963860)
XLA Ops:
  0.6 76.8 %stack.1 = (f32[1,1]{1,0:T(1,128)}, bf16[8192,512]{1,0:T(8,128)(2,1)S(1)}, f32[32,512]{1,0:T(8,128)S(1)}, f32[32,1024]{1,0:T(8,128)S(1)}, f32[32,1024]{1,0:T(8,1...) custom-call(bf16[8192,512]{1,0:T(8,128)(2,1)} %acts_hbm.1, ...), custom_call_target="tpu_custom_call" | custom-call | tf_op jit(solution)/shard_map/stack/pallas_call | solution.py:703
  77.5 4.2 %emit.1 = (f32[1]{0:T(128)}, bf16[8192,512]{1,0:T(8,128)(2,1)}, f32[32,512]{1,0:T(8,128)}, f32[32,1024]{1,0:T(8,128)}, f32[32,1024]{1,0:T(8,128)}, /*index=5*/f3...) custom-call(f32[1,1]{1,0:T(1,128)} %get-tuple-element.24.refs_0_, ...), custom_call_target="tpu_custom_call" | custom-call | tf_op jit(solution)/shard_map/emit/pallas_call | solution.py:715

commit v6 on v5

--- a/solution.py
+++ b/solution.py
@@ -473,6 +473,19 @@
         (un0_ref, un1_ref, un2_ref)[i][...] = own[0:1]
         (v0_ref, v1_ref, v2_ref)[i][...] = v16[0:1]
 
+    def products(w_ref, xt_ref, y_ref):
+        for j in range(width // FTILE):
+            at = pl.ds(j * FTILE, FTILE)
+            y_ref[at, :] = dot(w_ref[at, :], xt_ref[...], NN)
+
+    def scaled(inv, y_ref, next_ref, mask_ref):
+        for j in range(width // FTILE):
+            at = pl.ds(j * FTILE, FTILE)
+            y = y_ref[at, :] * inv
+            y_ref[at, :] = y
+            next_ref[at, :] = jnp.where(y >= 0, y, LEAK * y).astype(BF16)
+            mask_ref[at, :] = jnp.where(y >= 0, 1.0, 0.0).astype(BF16)
+
     def forward(w_ref, xt_ref, inv, y_ref, next_ref, mask_ref):
         for j in range(width // FTILE):
             at = pl.ds(j * FTILE, FTILE)
@@ -496,27 +509,28 @@
     gb.step3()
     ga.step4()
     gc.step3()
+    spread.first_relay()
     gb.step4()
-    spread.first_relay()
     ga.finish()
     start_rows()
     power(0, w0, ustart[0:1, :])
     gc.step4()
+    spread.second_send()
     sa = sigma_of(0)
     inva = 1.0 / sa
     forward(w0, xt0, inva, yt0, xt1, mt)
     turn(mt, mask0)
-    spread.second_send()
     gb.finish()
     gc.finish()
     power(1 + p.core, wb.at[p.core], jnp.where(p.core == 0, ustart[1:2, :], ustart[2:3, :]))
     other = Link(p, send_sems.at[10 + DX_PARTS], o_recv)
     other.start(0, uv.at[1 + p.core], uv.at[1 + p.core], p.mate())
     spread.second_relay()
+    products(w1, xt1, yt1)
     other.wait(0, uv.at[2 - p.core])
     sb, sc = sigma_of(1), sigma_of(2)
     invb = 1.0 / sb
-    forward(w1, xt1, invb, yt1, xt2, mt)
+    scaled(invb, yt1, xt2, mt)
     invc = 1.0 / sc
     forward(w2, xt2, invc, yt2, None, None)
     turn(mt, mask1)

time: 81.9 us -> 81.6 us (level)
  no operation moved by 1% of the time
where the time goes in v6:
time: 81.6 us; the launch traced here: 81.5 us
  Pallas kernels  80.7 us (99%)
  between operations  0.82 us (1%)
    pallas_call x1, Pallas kernels, device_program(): pl.pallas_call(functools.partial(kernel, n), out_shape=out_shape, in_spec...  76.5 us
    pallas_call x1, Pallas kernels, device_program(): pl.pallas_call(functools.partial(emit, len(final)), out_shape=final, in_s...  4.16 us

profile of v6, /device:TPU:97, one launch (start us, length us, event | category | flops | bytes accessed | tf_op | source)
XLA Modules:
  0.0 81.5 jit_solution(12119637047442768689)
XLA Ops:
  0.6 76.5 %stack.1 = (f32[1,1]{1,0:T(1,128)}, bf16[8192,512]{1,0:T(8,128)(2,1)S(1)}, f32[32,512]{1,0:T(8,128)S(1)}, f32[32,1024]{1,0:T(8,128)S(1)}, f32[32,1024]{1,0:T(8,1...) custom-call(bf16[8192,512]{1,0:T(8,128)(2,1)} %acts_hbm.1, ...), custom_call_target="tpu_custom_call" | custom-call | tf_op jit(solution)/shard_map/stack/pallas_call | solution.py:717
  77.2 4.2 %emit.1 = (f32[1]{0:T(128)}, bf16[8192,512]{1,0:T(8,128)(2,1)}, f32[32,512]{1,0:T(8,128)}, f32[32,1024]{1,0:T(8,128)}, f32[32,1024]{1,0:T(8,128)}, /*index=5*/f3...) custom-call(f32[1,1]{1,0:T(1,128)} %get-tuple-element.24.refs_0_, ...), custom_call_target="tpu_custom_call" | custom-call | tf_op jit(solution)/shard_map/emit/pallas_call | solution.py:729
